TPU v7x, 32 devices: a whole 2x2x4 slice. The times are simulated.
32 devices in a mesh: model: 4 (over z), data: 8 (over y, x, core).
Axes of the slice: x: 2, y: 2, z: 4, core: 2. Of those that a mesh axis runs over, the one named last changes fastest.
Arguments:
- grad_wi0: float32 [8, 1024, 2816], P('data', None, 'model')
- param_wi0: float32 [1024, 2816], P('data', 'model')
- vrow_wi0: float32 [1024], P('data')
- vcol_wi0: float32 [2816], P('model')
- grad_wi1: float32 [8, 1024, 2816], P('data', None, 'model')
- param_wi1: float32 [1024, 2816], P('data', 'model')
- vrow_wi1: float32 [1024], P('data')
- vcol_wi1: float32 [2816], P('model')
- grad_wo: float32 [8, 2816, 1024], P('data', None, 'model')
- param_wo: float32 [2816, 1024], P('data', 'model')
- vrow_wo: float32 [2816], P('data')
- vcol_wo: float32 [1024], P('model')
- grad_wq: float32 [8, 1024, 1024], P('data', None, 'model')
- param_wq: float32 [1024, 1024], P('data', 'model')
- vrow_wq: float32 [1024], P('data')
- vcol_wq: float32 [1024], P('model')
Outputs:
- output 1: float32 [1024, 2816], P('data', 'model')
- output 2: float32 [1024, 2816], P('data', 'model')
- output 3: float32 [1024], P('data')
- output 4: float32 [2816], P('model')
- output 5: float32 [1024, 2816], P('data', 'model')
- output 6: float32 [1024, 2816], P('data', 'model')
- output 7: float32 [1024], P('data')
- output 8: float32 [2816], P('model')
- output 9: float32 [2816, 1024], P('data', 'model')
- output 10: float32 [2816, 1024], P('data', 'model')
- output 11: float32 [2816], P('data')
- output 12: float32 [1024], P('model')
- output 13: float32 [1024, 1024], P('data', 'model')
- output 14: float32 [1024, 1024], P('data', 'model')
- output 15: float32 [1024], P('data')
- output 16: float32 [1024], P('model')
All inputs are finite; a program needn't handle non-finite values.
Results may differ from a plain program's by a relative error of at most 0.001.
Values sent between devices are 32-bit elements.
A program may use at most 1 GiB of HBM per device.

v0:
```python
import jax
import jax.numpy as jnp
from jax import lax
from jax.sharding import PartitionSpec as P

OPT_STEP = 3
MATRICES = 4


def shard_update(grad_rep, param, vrow, vcol, n_data, n_model):
    decay_pow = OPT_STEP ** -0.8
    beta = 1.0 - decay_pow
    step_pow = OPT_STEP ** -0.5
    lr_rel = min(0.01, step_pow)
    rows_total = param.shape[0] * n_data
    cols_total = param.shape[1] * n_model
    entries = rows_total * cols_total
    grad_sum = lax.psum_scatter(grad_rep[0], 'data', scatter_dimension=0, tiled=True)
    grad_sq = grad_sum * grad_sum + 1e-30
    row_mean = lax.psum(jnp.sum(grad_sq, axis=1), 'model') / cols_total
    col_mean = lax.psum(jnp.sum(grad_sq, axis=0), 'data') / rows_total
    vrow_new = beta * vrow + (1.0 - beta) * row_mean
    vcol_new = beta * vcol + (1.0 - beta) * col_mean
    vrow_avg = lax.psum(jnp.sum(vrow_new), 'data') / rows_total
    row_factor = lax.rsqrt(vrow_new / vrow_avg)
    col_factor = lax.rsqrt(vcol_new)
    update = grad_sum * row_factor[:, None] * col_factor[None, :]
    update_rms = jnp.sqrt(lax.psum(jnp.sum(update * update), ('model', 'data')) / entries)
    param_rms = jnp.sqrt(lax.psum(jnp.sum(param * param), ('model', 'data')) / entries)
    update = update / jnp.maximum(1.0, update_rms)
    delta = -(lr_rel * jnp.maximum(1e-3, param_rms)) * update
    return param + delta, delta, vrow_new, vcol_new


def solution(mesh):
    n_data = mesh.shape['data']
    n_model = mesh.shape['model']
    mat_spec = P('data', 'model')
    in_specs = (P('data', None, 'model'), mat_spec, P('data'), P('model')) * MATRICES
    out_specs = (mat_spec, mat_spec, P('data'), P('model')) * MATRICES

    def per_device(*arrays):
        results = []
        for index in range(MATRICES):
            grad_rep, param, vrow, vcol = arrays[4 * index:4 * index + 4]
            results.extend(shard_update(grad_rep, param, vrow, vcol, n_data, n_model))
        return tuple(results)

    return jax.shard_map(per_device, mesh=mesh, in_specs=in_specs, out_specs=out_specs, check_vma=False)
```

profile of v0, /device:TPU:0, one launch (start us, length us, event | category | flops | bytes accessed | tf_op | source)
XLA Modules:
  0.0 297.5 jit_solution(4304909537207208767)
XLA Ops:
  7.2 0.0 reduce-scatter.11.cloned.1.call-start
  7.2 0.7 reduce-scatter.11.cloned.1.call-update
  7.9 0.0 reduce-scatter.5.cloned.1.call-start
  8.0 0.7 reduce-scatter.5.cloned.1.call-update
  8.7 0.0 reduce-scatter.7.cloned.1.call-start
  8.7 0.0 copy-start.6
  8.7 0.0 copy-start.4
  8.7 0.0 copy-start.2
  8.7 0.0 copy-start.3
  8.8 0.6 reduce-scatter.7.cloned.1.call-update
  9.4 0.0 copy-start.13
  9.4 0.0 copy-start.10
  9.4 0.0 copy-start.15
  9.4 0.0 copy-start.16
  9.4 0.0 copy-start.8
  9.5 0.0 copy-start.9
  9.5 0.0 copy-start.11
  9.5 0.0 copy-start.12
  9.5 0.0 reduce-scatter.9.cloned.1.call-start
  9.5 0.5 reduce-scatter.9.cloned.1.call-update
  10.1 0.0 copy-done.6
  10.1 0.6 multiply_reduce_fusion.7
  10.7 0.0 copy-done.4
  10.7 0.7 multiply_reduce_fusion.1
  11.4 0.0 copy-done.2
  11.4 0.0 copy-done.3
  11.4 0.7 multiply_reduce_fusion.3
  12.1 37.7 %reduce-scatter.11.cloned.1.call-done = f32[128,256]{1,0:T(8,128)} async-done(((f32[1024,256]{1,0:T(8,128)}), f32[128,256]{1,0:T(8,128)}) %reduce-scatter.11.cloned.1.call-update) | async-done | bytes 131088 | tf_op jit(solution)/shard_map/reduce_scatter | solution.py:18
  49.8 1.0 fusion.7
  50.8 46.9 %reduce-scatter.5.cloned.1.call-done = f32[128,704]{0,1:T(8,128)} async-done(((f32[1024,704]{0,1:T(8,128)}), f32[128,704]{0,1:T(8,128)}) %reduce-scatter.5.cloned.1.call-update) | async-done | bytes 360464 | tf_op jit(solution)/shard_map/reduce_scatter | solution.py:18
  97.7 1.2 fusion.1
  98.9 46.7 %reduce-scatter.7.cloned.1.call-done = f32[128,704]{0,1:T(8,128)} async-done(((f32[1024,704]{0,1:T(8,128)}), f32[128,704]{0,1:T(8,128)}) %reduce-scatter.7.cloned.1.call-update) | async-done | bytes 360464 | tf_op jit(solution)/shard_map/reduce_scatter | solution.py:18
  145.6 1.2 fusion.3
  146.9 46.5 %reduce-scatter.9.cloned.1.call-done = f32[352,256]{1,0:T(8,128)} async-done(((f32[2816,256]{1,0:T(8,128)}), f32[352,256]{1,0:T(8,128)}) %reduce-scatter.9.cloned.1.call-update) | async-done | bytes 360464 | tf_op jit(solution)/shard_map/reduce_scatter | solution.py:18
  193.4 1.2 fusion.5
  194.6 11.7 %all-reduce.2 = (f32[128]{0:T(128)S(1)}, f32[128]{0:T(128)S(1)}, f32[352]{0:T(512)S(1)}, f32[128]{0:T(128)S(1)}) all-reduce(f32[128]{0:T(128)S(1)} %get-tuple-element.20, f32[128]{0:T(128)S(1)} %get-tuple-element.18, f32[352]{0:T(512)S(1)} %get-tuple-element.16, ...), channel_id=1, replica_groups=mesh['model'=4,'data'=8] {'model'}, use_global_device_ids=true, to_apply=%region_4.0 | all-reduce | flops 736 | bytes 5888 | tf_op jit(solution)/shard_map/psum | solution.py:20
  206.3 0.0 copy-done.13
  206.3 0.6 fusion.19
  206.9 0.0 copy-done.10
  206.9 0.6 fusion.17
  207.5 0.0 copy-done.15
  207.5 0.0 copy-done.16
  207.5 0.6 fusion.16
  208.1 22.5 %all-reduce.1 = (f32[704]{0:T(1024)S(1)}, f32[]{:T(128)}, f32[704]{0:T(1024)S(1)}, f32[]{:T(128)}, f32[256]{0:T(256)S(1)}, /*index=5*/f32[]{:T(128)}, f32[256]{0:T(256)S(1)}, f32[]{:T(128)}) all-reduce(f32[704]{0:T(1024)S(1)} %get-tuple-element.21, f32[]{:T(128)} %get-tuple-element.66, ...), channel_id=1, replica_groups=mesh['model'=4,'data'=8] {'data'}, use_global_device_ids=true, to_apply=%region_8.0 | all-reduce | flops 1924 | bytes 15392 | tf_op jit(solution)/shard_map/psum | solution.py:21
  232.6 0.0 copy-done.8
  232.6 0.6 fusion.15
  233.2 0.0 copy-done.9
  233.2 0.6 fusion.14
  233.8 0.0 copy-done.11
  233.8 0.6 fusion.13
  235.0 0.0 copy-done.12
  235.0 0.6 fusion.12
  235.6 1.8 multiply_reduce_fusion.4
  237.4 1.8 multiply_reduce_fusion.2
  239.1 1.8 multiply_reduce_fusion
  240.9 1.6 multiply_reduce_fusion.6
  242.5 38.0 %all-reduce = (f32[]{:T(128)}, f32[]{:T(128)}, f32[]{:T(128)}, f32[]{:T(128)}, f32[]{:T(128)}, /*index=5*/f32[]{:T(128)}, f32[]{:T(128)}, f32[]{:T(128)}) all-reduce(f32[]{:T(128)} %multiply_reduce_fusion.4, f32[]{:T(128)} %get-tuple-element.71, f32[]{:T(128)} %multiply_reduce_fusion.2, ...), channel_id=1, replica_groups=mesh['model'=4,'data'=8] {'model','data'}, use_global_device_ids=true, to_apply=%region_10.0 | all-reduce | flops 8 | bytes 64 | tf_op jit(solution)/shard_map/psum | solution.py:28
  286.1 2.0 fusion.11
  288.1 0.0 copy-done
  288.1 1.0 fusion.10
  289.1 0.0 copy-done.1
  289.1 1.0 fusion.9
  290.1 0.0 copy-done.7
  290.1 0.8 fusion.8
  (15 shorter events, 0.0 us)
Async XLA Ops:
  7.2 42.7 %reduce-scatter.11.cloned.1.call-start = ((), (), s32[]{:S(2)}) async-start(), calls=%async_computation.7 | async-start | bytes 1179648 | tf_op jit(solution)/shard_map/reduce_scatter | solution.py:18
  7.9 89.8 %reduce-scatter.5.cloned.1.call-start = ((), (), s32[]{:S(2)}) async-start(), calls=%async_computation.4 | async-start | bytes 3244032 | tf_op jit(solution)/shard_map/reduce_scatter | solution.py:18
  8.7 137.0 %reduce-scatter.7.cloned.1.call-start = ((), (), s32[]{:S(2)}) async-start(), calls=%async_computation.5 | async-start | bytes 3244032 | tf_op jit(solution)/shard_map/reduce_scatter | solution.py:18
  8.7 1.3 copy-start.6
  8.7 2.0 copy-start.4
  8.7 2.7 copy-start.2
  8.7 2.7 copy-start.3
  9.4 196.9 %copy-start.13 = (f32[128]{0:T(128)S(1)}, f32[128]{0:T(128)}, u32[]{:S(2)}) copy-start(f32[128]{0:T(128)} %param.18) | copy-start | bytes 1540
  9.4 197.5 %copy-start.10 = (f32[352]{0:T(512)S(1)}, f32[352]{0:T(512)}, u32[]{:S(2)}) copy-start(f32[352]{0:T(512)} %param.26) | copy-start | bytes 4228
  9.4 198.1 %copy-start.15 = (f32[128]{0:T(128)S(1)}, f32[128]{0:T(128)}, u32[]{:S(2)}) copy-start(f32[128]{0:T(128)} %param.30) | copy-start | bytes 1540
  9.4 198.1 %copy-start.16 = (f32[128]{0:T(128)S(1)}, f32[128]{0:T(128)}, u32[]{:S(2)}) copy-start(f32[128]{0:T(128)} %param.22) | copy-start | bytes 1540
  9.4 223.1 %copy-start.8 = (f32[704]{0:T(1024)S(1)}, f32[704]{0:T(1024)}, u32[]{:S(2)}) copy-start(f32[704]{0:T(1024)} %param.19) | copy-start | bytes 8452
  9.5 223.7 %copy-start.9 = (f32[704]{0:T(1024)S(1)}, f32[704]{0:T(1024)}, u32[]{:S(2)}) copy-start(f32[704]{0:T(1024)} %param.23) | copy-start | bytes 8452
  9.5 224.3 %copy-start.11 = (f32[256]{0:T(256)S(1)}, f32[256]{0:T(256)}, u32[]{:S(2)}) copy-start(f32[256]{0:T(256)} %param.27) | copy-start | bytes 3076
  9.5 225.6 %copy-start.12 = (f32[256]{0:T(256)S(1)}, f32[256]{0:T(256)}, u32[]{:S(2)}) copy-start(f32[256]{0:T(256)} %param.31) | copy-start | bytes 3076
  9.5 183.9 %reduce-scatter.9.cloned.1.call-start = ((), (), s32[]{:S(2)}) async-start(), calls=%async_computation.6 | async-start | bytes 3244032 | tf_op jit(solution)/shard_map/reduce_scatter | solution.py:18
  145.6 142.4 %copy-start = (f32[128,704]{0,1:T(8,128)S(1)}, f32[128,704]{0,1:T(8,128)}, u32[]{:S(2)}) copy-start(f32[128,704]{0,1:T(8,128)} %reduce-scatter.7.cloned.1.call-done) | copy-start | bytes 1081348
  193.4 95.7 %copy-start.1 = (f32[352,256]{1,0:T(8,128)S(1)}, f32[352,256]{1,0:T(8,128)}, u32[]{:S(2)}) copy-start(f32[352,256]{1,0:T(8,128)} %reduce-scatter.9.cloned.1.call-done) | copy-start | bytes 1081348
  206.9 83.2 %copy-start.14 = (f32[128]{0:T(128)}, f32[128]{0:T(128)S(1)}, u32[]{:S(2)}) copy-start(f32[128]{0:T(128)S(1)} %get-tuple-element.67) | copy-start | bytes 1540
  207.5 82.6 %copy-start.7 = (f32[352]{0:T(512)}, f32[352]{0:T(512)S(1)}, u32[]{:S(2)}) copy-start(f32[352]{0:T(512)S(1)} %get-tuple-element.63) | copy-start | bytes 4228
  208.1 82.0 %copy-start.17 = (f32[128]{0:T(128)}, f32[128]{0:T(128)S(1)}, u32[]{:S(2)}) copy-start(f32[128]{0:T(128)S(1)} %get-tuple-element.61) | copy-start | bytes 1540
  208.1 82.0 %copy-start.18 = (f32[128]{0:T(128)}, f32[128]{0:T(128)S(1)}, u32[]{:S(2)}) copy-start(f32[128]{0:T(128)S(1)} %get-tuple-element.69) | copy-start | bytes 1540
  208.1 82.0 %copy-start.5 = (f32[128,256]{1,0:T(8,128)S(1)}, f32[128,256]{1,0:T(8,128)}, u32[]{:S(2)}) copy-start(f32[128,256]{1,0:T(8,128)} %reduce-scatter.11.cloned.1.call-done) | copy-start | bytes 393220
Sparse Core Ops, SparseCore 0:
  11.2 38.6 reduce-scatter.10
  53.2 44.4 reduce-scatter.4
  101.1 44.4 reduce-scatter.6
  148.9 44.4 reduce-scatter.8
where the time goes:
time: 299 us; the launch traced here: 297 us
  waiting for transfers between devices  180 us (60%)
  blocking collectives  72.2 us (24%)
  other arithmetic  22.5 us (8%)
  between operations  22.1 us (7%)
    reduce_scatter x4, waiting for transfers between devices, shard_update(): lax.psum_scatter(grad_rep[0], 'data', scatter_dimension=0, tiled=True)  178 us
    psum x1, blocking collectives, shard_update(): lax.psum(jnp.sum(update * update), ('model', 'data')) / entries  38 us
    psum x1, blocking collectives, shard_update(): col_mean = lax.psum(jnp.sum(grad_sq, axis=0), 'data') / rows_total  22.5 us
    psum x1, blocking collectives, shard_update(): row_mean = lax.psum(jnp.sum(grad_sq, axis=1), 'model') / cols_total  11.7 us
    reduce_sum x4, other arithmetic, shard_update(): jnp.sum(update * update)  6.88 us
  transfers between devices with their start and end apart: 4, of which 4 were waited for; matrix products, arithmetic and copies ran while one was open for 2% of the time, Pallas kernels for 0%

commit v1 on v0

v1 whole, which is shorter than its diff:
```python
import jax
import jax.numpy as jnp
from jax import lax
from jax.experimental import pallas as pl
from jax.experimental.pallas import tpu as pltpu
from jax.sharding import PartitionSpec as P

OPT_STEP = 3
BETA = 1.0 - OPT_STEP ** -0.8
LR_REL = min(0.01, OPT_STEP ** -0.5)
NM = 4
OWN, NX, NY, ND = 0, 1, 2, 3
STEP_ROWS = (32, 32, 88, 64)
MESH_ID = pl.DeviceIdType.MESH


def make_reduce_kernel(rows_b, cols, n_model, n_data):
    rh = [r // 2 for r in rows_b]
    tiles = [-(-c // 128) for c in cols]
    vtiles = [-(-r // 128) for r in rows_b]
    rows_t = [r * n_data for r in rows_b]
    cols_t = [c * n_model for c in cols]

    def kernel(*refs):
        grads = refs[0:4]
        params = refs[4:8]
        vrows = refs[8:12]
        vcols = refs[12:16]
        upd = refs[16:20]
        vrow_out = refs[20:24]
        vcol_out = refs[24:28]
        fac_out = refs[28]
        sc = list(refs[29:])
        take = lambda n: [sc.pop(0) for _ in range(n)]
        loc, rec, fx, fy, wbuf, vrbuf, vcbuf, crow = (take(4) for _ in range(8))
        rmsg, rrx, cmsg, crx, bmsg, brx, vrc, vcc, w2 = take(9)
        (ld_sem, dd_s, dd_r, x_s, x_r, y_s, y_r, in_sem,
         ra_s, ra_r, ca_s, ca_r, b_s, b_r) = take(14)
        greet = take(1)[0]

        z = lax.axis_index('model')
        d = lax.axis_index('data')
        core = lax.rem(d, 2)
        xx = lax.rem(d // 2, 2)
        yy = d // 4
        sib = d + 1 - 2 * core
        dx = d + 2 - 4 * xx
        dy = d + 4 - 8 * yy
        dd = dx + 4 - 8 * yy
        owner = {OWN: d, NX: dx, NY: dy, ND: dd}
        flip = 1 - 2 * core

        lane = lax.broadcasted_iota(jnp.int32, (8, 128), 1)
        sub = lax.broadcasted_iota(jnp.int32, (8, 128), 0)

        def remote(src, dst, ssem, rsem, data=None, model=None):
            return pltpu.make_async_remote_copy(
                src_ref=src, dst_ref=dst, send_sem=ssem, recv_sem=rsem,
                device_id=(z if model is None else model, d if data is None else data),
                device_id_type=MESH_ID)

        def signal(sem, data=None, model=None):
            pl.semaphore_signal(
                sem, inc=1,
                device_id=(z if model is None else model, d if data is None else data),
                device_id_type=MESH_ID)

        order = []
        for m in range(NM):
            order += [(m, ND, 0), (m, ND, 1), (m, NX, 0), (m, NY, 1)]
        for m in range(NM):
            order += [(m, NY, 0), (m, NX, 1)]
        for m in range(NM):
            order += [(m, OWN, 0), (m, OWN, 1)]

        def slot(m, j, h):
            return (m * 4 + j) * 2 + h

        loads = {}
        for m, j, h in order:
            start = pl.multiple_of(owner[j] * rows_b[m] + h * rh[m], 8)
            loads[m, j, h] = pltpu.make_async_copy(
                grads[m].at[0, pl.ds(start, rh[m]), :], loc[m].at[j, h], ld_sem.at[slot(m, j, h)])
            loads[m, j, h].start()
        small = []
        for m in range(NM):
            small.append(pltpu.make_async_copy(params[m], wbuf[m], in_sem.at[m]))
            small.append(pltpu.make_async_copy(vrows[m], vrbuf[m], in_sem.at[4 + m]))
            small.append(pltpu.make_async_copy(vcols[m], vcbuf[m], in_sem.at[8 + m]))
        for cp in small:
            cp.start()

        barrier = pltpu.get_barrier_semaphore()
        for peer in (sib, dx, dy):
            signal(barrier, data=peer)
        up_ok = z < n_model - 1
        down_ok = z > 0

        def signal_z(sem):
            @pl.when(up_ok)
            def _():
                signal(sem, model=z + 1)

            @pl.when(down_ok)
            def _():
                signal(sem, model=z - 1)

        n_z = jnp.where(up_ok, 1, 0) + jnp.where(down_ok, 1, 0)
        signal_z(barrier)
        pl.semaphore_wait(barrier, 3 + n_z)

        dsend = {}
        for m, j, h in order:
            start = pl.multiple_of((owner[j] + flip) * rows_b[m] + h * rh[m], 8)
            k = slot(m, j, h)
            dsend[m, j, h] = remote(
                grads[m].at[0, pl.ds(start, rh[m]), :], rec[m].at[j, h], dd_s.at[k], dd_r.at[k], data=sib)
            dsend[m, j, h].start()

        def pair_sum(m, j, h, extra=None):
            loads[m, j, h].wait()
            dsend[m, j, h].wait_recv()
            total = loc[m][j, h] + rec[m][j, h]
            if extra is not None:
                total = total + extra
            loc[m][j, h] = total

        xsend, ysend = {}, {}
        for m in range(NM):
            xsend[m, 0] = remote(loc[m].at[ND, 0], fx[m].at[0], x_s.at[3 * m], x_r.at[3 * m], data=dx)
            xsend[m, 1] = remote(loc[m].at[NX, 0], fx[m].at[1], x_s.at[3 * m + 1], x_r.at[3 * m + 1], data=dx)
            xsend[m, 2] = remote(loc[m].at[NX, 1], fx[m].at[2], x_s.at[3 * m + 2], x_r.at[3 * m + 2], data=dx)
            ysend[m, 0] = remote(loc[m].at[ND, 1], fy[m].at[0], y_s.at[3 * m], y_r.at[3 * m], data=dy)
            ysend[m, 1] = remote(loc[m].at[NY, 0], fy[m].at[1], y_s.at[3 * m + 1], y_r.at[3 * m + 1], data=dy)
            ysend[m, 2] = remote(loc[m].at[NY, 1], fy[m].at[2], y_s.at[3 * m + 2], y_r.at[3 * m + 2], data=dy)

        for m in range(NM):
            pair_sum(m, ND, 0)
            xsend[m, 0].start()
            pair_sum(m, ND, 1)
            ysend[m, 0].start()
            pair_sum(m, NX, 0)
            xsend[m, 1].start()
            pair_sum(m, NY, 1)
            ysend[m, 2].start()

        for cp in small:
            cp.wait()
        w2v = jnp.zeros((8, 128), jnp.float32)
        for m in range(NM):
            w = wbuf[m][...]
            part = jnp.sum(w * w, axis=(0, 1), keepdims=True) * (1.0 / (rows_t[m] * cols_t[m]))
            w2v = jnp.where((sub == 2) & (lane == m), part, w2v)
            cmsg[m] = jnp.zeros((8, 128), jnp.float32)
            vcc[m] = jnp.ones((8, 128), jnp.float32)
            for k in range(tiles[m]):
                w_k = min(128, cols[m] - 128 * k)
                vcc[m, k:k + 1, 0:w_k] = vcbuf[m][0:1, 128 * k:128 * k + w_k]
            acc = jnp.zeros((8, 128), jnp.float32)
            for t in range(vtiles[m]):
                n_t = min(128, rows_b[m] - 128 * t)
                row = jnp.broadcast_to(vrbuf[m][t:t + 1, :], (8, 128))
                for g in range(n_t // 8):
                    col = jnp.sum(jnp.where(lane == 8 * g + sub, row, 0.0), axis=1, keepdims=True)
                    acc = jnp.where(lane == 16 * t + g, col, acc)
            vrc[m] = acc
        w2[...] = w2v

        signal(greet.at[0], data=sib)
        pl.semaphore_wait(greet.at[0], 1)
        signal(greet.at[1], data=dx)
        pl.semaphore_wait(greet.at[1], 1)
        signal(greet.at[2], data=dy)
        pl.semaphore_wait(greet.at[2], 1)
        signal_z(greet.at[3])
        pl.semaphore_wait(greet.at[3], n_z)
        signal_z(greet.at[4])
        pl.semaphore_wait(greet.at[4], n_z)

        for m in range(NM):
            xsend[m, 0].wait_recv()
            pair_sum(m, NY, 0, fx[m][0])
            ysend[m, 1].start()
            ysend[m, 0].wait_recv()
            pair_sum(m, NX, 1, fy[m][0])
            xsend[m, 2].start()

        rsend, csend = {}, {}
        for m in range(NM):
            for k in range(1, n_model):
                i = m * (n_model - 1) + k - 1
                rsend[m, k] = remote(rmsg.at[m], rrx.at[i], ra_s.at[i], ra_r.at[i],
                                     model=lax.rem(z + k, n_model))
            for k in range(1, n_data):
                i = m * (n_data - 1) + k - 1
                csend[m, k] = remote(cmsg.at[m], crx.at[i], ca_s.at[i], ca_r.at[i],
                                     data=lax.rem(d + k, n_data))

        for m in range(NM):
            step = STEP_ROWS[m]
            cacc = jnp.zeros((8, cols[m]), jnp.float32)
            racc = jnp.zeros((8, 128), jnp.float32)
            for h in range(2):
                loads[m, OWN, h].wait()
                dsend[m, OWN, h].wait_recv()
                xsend[m, 1 + h].wait_recv()
                ysend[m, 1 + h].wait_recv()

                def body(it, carry, m=m, h=h, step=step):
                    cacc, racc = carry
                    r0 = pl.multiple_of(it * step, 8)
                    rows = pl.ds(r0, step)
                    total = (loc[m][OWN, h, rows, :] + rec[m][OWN, h, rows, :]
                             + fx[m][1 + h, rows, :] + fy[m][1 + h, rows, :])
                    upd[m][pl.ds(pl.multiple_of(h * rh[m] + r0, 8), step), :] = total
                    sq = total * total + 1e-30
                    for g in range(step // 8):
                        part = sq[8 * g:8 * g + 8, :]
                        cacc = cacc + part
                        rsum = jnp.sum(part, axis=1, keepdims=True)
                        racc = jnp.where(lane == (h * rh[m] + it * step) // 8 + g, rsum, racc)
                    return cacc, racc

                cacc, racc = lax.fori_loop(0, rh[m] // step, body, (cacc, racc))
            rmsg[m] = racc
            csum = jnp.sum(cacc, axis=0, keepdims=True)
            for k in range(tiles[m]):
                w_k = min(128, cols[m] - 128 * k)
                cmsg[m, k:k + 1, 0:w_k] = csum[:, 128 * k:128 * k + w_k]
            for k in range(1, n_model):
                rsend[m, k].start()
            for k in range(n_data - 1, 0, -1):
                csend[m, k].start()

        bv = w2[...]
        locrow = jnp.ones((8, 128), jnp.float32)
        for m in range(NM):
            rtot = rmsg[m]
            for k in range(1, n_model):
                rsend[m, k].wait_recv()
                rtot = rtot + rrx[m * (n_model - 1) + k - 1]
            ctot = cmsg[m]
            for k in range(1, n_data):
                csend[m, k].wait_recv()
                ctot = ctot + crx[m * (n_data - 1) + k - 1]
            vr = BETA * vrc[m] + (1.0 - BETA) * (rtot * (1.0 / cols_t[m]))
            vc = BETA * vcc[m] + (1.0 - BETA) * (ctot * (1.0 / rows_t[m]))
            vrc[m] = vr
            valid = lane < rows_b[m] // 8
            vr_sum = jnp.sum(jnp.where(valid, vr, 0.0), axis=(0, 1), keepdims=True)
            mloc = vr_sum * (1.0 / rows_b[m])
            rfac = lax.rsqrt(jnp.where(valid, vr / mloc, 1.0))
            cfac = lax.rsqrt(vc)
            for k in range(tiles[m]):
                w_k = min(128, cols[m] - 128 * k)
                crow[m][0:1, 128 * k:128 * k + w_k] = cfac[k:k + 1, 0:w_k]
                vcol_out[m][0:1, 128 * k:128 * k + w_k] = vc[k:k + 1, 0:w_k]
            cf = jnp.broadcast_to(crow[m][0:1, :], (8, cols[m]))
            step = STEP_ROWS[m]

            def tbody(it, tacc, m=m, step=step, cf=cf, rfac=rfac):
                for g in range(step // 8):
                    r0 = pl.multiple_of(it * step + 8 * g, 8)
                    rcol = jnp.sum(jnp.where(lane == it * (step // 8) + g, rfac, 0.0), axis=1, keepdims=True)
                    u = upd[m][pl.ds(r0, 8), :] * rcol * cf
                    upd[m][pl.ds(r0, 8), :] = u
                    tacc = tacc + u * u
                return tacc

            tacc = lax.fori_loop(0, rows_b[m] // step, tbody, jnp.zeros((8, cols[m]), jnp.float32))
            t_m = jnp.sum(tacc, axis=(0, 1), keepdims=True) * (1.0 / (rows_t[m] * cols_t[m]))
            bv = jnp.where((sub == 0) & (lane == m), t_m / mloc, bv)
            bv = jnp.where((sub == 1) & (lane == m), vr_sum * (1.0 / (rows_t[m] * n_model)), bv)
            locrow = jnp.where(lane == m, mloc, locrow)

        bmsg[...] = bv
        bsend = []
        for kz in range(n_model):
            for kd in range(n_data):
                if kz == 0 and kd == 0:
                    continue
                i = kz * n_data + kd - 1
                bsend.append(remote(bmsg, brx.at[i], b_s.at[i], b_r.at[i],
                                    data=lax.rem(d + kd, n_data), model=lax.rem(z + kz, n_model)))
        for cp in reversed(bsend):
            cp.start()

        for m in range(NM):
            vr = vrc[m]
            for t in range(vtiles[m]):
                n_t = min(128, rows_b[m] - 128 * t)
                acc = jnp.zeros((8, 128), jnp.float32)
                for g in range(n_t // 8):
                    col = jnp.sum(jnp.where(lane == 16 * t + g, vr, 0.0), axis=1, keepdims=True)
                    acc = jnp.where(lane == 8 * g + sub, col, acc)
                keep = jnp.where(lax.rem(lane, 8) == sub, acc, 0.0)
                vrow_out[m][t:t + 1, :] = jnp.sum(keep, axis=0, keepdims=True)

        for cp in bsend:
            cp.wait_recv()
        tot = bmsg[...]
        for i in range(n_model * n_data - 1):
            tot = tot + brx[i]
        mean_vr = tot[1:2, :]
        u_rms = jnp.sqrt(mean_vr * tot[0:1, :])
        w_rms = jnp.sqrt(tot[2:3, :])
        fac = -(LR_REL * jnp.maximum(1e-3, w_rms)) * (jnp.sqrt(mean_vr) * lax.rsqrt(locrow[0:1, :]))
        fac_out[...] = jnp.broadcast_to(fac / jnp.maximum(1.0, u_rms), (8, 128))

        for key in dsend:
            dsend[key].wait_send()
        for group in (xsend, ysend, rsend, csend):
            for key in group:
                group[key].wait_send()
        for cp in bsend:
            cp.wait_send()

    f32 = jnp.float32
    n_row_msgs = NM * (n_model - 1)
    n_col_msgs = NM * (n_data - 1)
    n_b = n_model * n_data - 1
    dma = pltpu.SemaphoreType.DMA
    scratch = []
    scratch += [pltpu.VMEM((4, 2, rh[m], cols[m]), f32) for m in range(NM)]
    scratch += [pltpu.VMEM((4, 2, rh[m], cols[m]), f32) for m in range(NM)]
    scratch += [pltpu.VMEM((3, rh[m], cols[m]), f32) for m in range(NM)]
    scratch += [pltpu.VMEM((3, rh[m], cols[m]), f32) for m in range(NM)]
    scratch += [pltpu.VMEM((rows_b[m], cols[m]), f32) for m in range(NM)]
    scratch += [pltpu.VMEM((vtiles[m], 128), f32) for m in range(NM)]
    scratch += [pltpu.VMEM((1, cols[m]), f32) for m in range(NM)]
    scratch += [pltpu.VMEM((1, cols[m]), f32) for m in range(NM)]
    scratch += [
        pltpu.VMEM((NM, 8, 128), f32), pltpu.VMEM((n_row_msgs, 8, 128), f32),
        pltpu.VMEM((NM, 8, 128), f32), pltpu.VMEM((n_col_msgs, 8, 128), f32),
        pltpu.VMEM((8, 128), f32), pltpu.VMEM((n_b, 8, 128), f32),
        pltpu.VMEM((NM, 8, 128), f32), pltpu.VMEM((NM, 8, 128), f32), pltpu.VMEM((8, 128), f32),
    ]
    scratch += [dma((32,)), dma((32,)), dma((32,)), dma((12,)), dma((12,)), dma((12,)), dma((12,)), dma((12,)),
                dma((n_row_msgs,)), dma((n_row_msgs,)), dma((n_col_msgs,)), dma((n_col_msgs,)),
                dma((n_b,)), dma((n_b,))]
    scratch += [pltpu.SemaphoreType.REGULAR((5,))]
    out_shape = ([jax.ShapeDtypeStruct((rows_b[m], cols[m]), f32) for m in range(NM)]
                 + [jax.ShapeDtypeStruct((vtiles[m], 128), f32) for m in range(NM)]
                 + [jax.ShapeDtypeStruct((1, cols[m]), f32) for m in range(NM)]
                 + [jax.ShapeDtypeStruct((8, 128), f32)])
    vmem = pl.BlockSpec(memory_space=pltpu.VMEM)
    anyspace = pl.BlockSpec(memory_space=pl.ANY)
    return pl.pallas_call(
        kernel, out_shape=out_shape, in_specs=[anyspace] * 16, out_specs=[vmem] * len(out_shape),
        scratch_shapes=scratch,
        compiler_params=pltpu.CompilerParams(collective_id=0, has_side_effects=True,
                                             vmem_limit_bytes=48 * 1024 * 1024))


def make_apply_kernel(rows_b, cols):
    def kernel(*refs):
        upd, params, vrow_in, vcol_in = refs[0:4], refs[4:8], refs[8:12], refs[12:16]
        fac_ref = refs[16]
        new, delta, vrow_out, vcol_out = refs[17:21], refs[21:25], refs[25:29], refs[29:33]
        for m in range(NM):
            fac = fac_ref[0:1, m:m + 1]
            step = fac * upd[m][...]
            delta[m][...] = step
            new[m][...] = params[m][...] + step
            vrow_out[m][...] = vrow_in[m][...]
            vcol_out[m][...] = vcol_in[m][...]

    f32 = jnp.float32
    vmem = pl.BlockSpec(memory_space=pltpu.VMEM)
    vtiles = [-(-r // 128) for r in rows_b]
    mats = [jax.ShapeDtypeStruct((rows_b[m], cols[m]), f32) for m in range(NM)]
    out_shape = (mats + mats + [jax.ShapeDtypeStruct((vtiles[m], 128), f32) for m in range(NM)]
                 + [jax.ShapeDtypeStruct((1, cols[m]), f32) for m in range(NM)])
    return pl.pallas_call(kernel, out_shape=out_shape, in_specs=[vmem] * 17, out_specs=[vmem] * 16)


def solution(mesh):
    n_data = mesh.shape['data']
    n_model = mesh.shape['model']
    mat_spec = P('data', 'model')
    in_specs = (P('data', None, 'model'), mat_spec, P('data'), P('model')) * NM
    out_specs = (mat_spec, mat_spec, P('data'), P('model')) * NM

    def per_device(*arrays):
        grads, params = arrays[0::4], arrays[1::4]
        rows_b = [p.shape[0] for p in params]
        cols = [p.shape[1] for p in params]
        vrows = [jnp.pad(v, (0, -v.shape[0] % 128)).reshape(-1, 128) for v in arrays[2::4]]
        vcols = [v.reshape(1, -1) for v in arrays[3::4]]
        outs = make_reduce_kernel(rows_b, cols, n_model, n_data)(*grads, *params, *vrows, *vcols)
        upd, vr, vc, fac = outs[0:4], outs[4:8], outs[8:12], outs[12]
        res = make_apply_kernel(rows_b, cols)(*upd, *params, *vr, *vc, fac)
        flat = []
        for m in range(NM):
            flat += [res[m], res[4 + m], res[8 + m].reshape(-1)[:rows_b[m]], res[12 + m].reshape(-1)]
        return tuple(flat)

    return jax.shard_map(per_device, mesh=mesh, in_specs=in_specs, out_specs=out_specs, check_vma=False)
```

time: 299 us -> 98.3 us (0.33)
  waiting for transfers between devices: 180 us -> 0 us
  blocking collectives: 72.2 us -> 0 us
  Pallas kernels: 0 us -> 66.9 us
  local copies, waits for them, and re-layouts: 0.08 us -> 27.4 us
  between operations: 22.1 us -> 0.82 us
  other arithmetic: 22.5 us -> 2.57 us
    reduce_scatter x4 -> x0, waiting for transfers between devices: 178 us -> none  [shard_update(): lax.psum_scatter(grad_rep[0], 'data', scatter_dimension=0, tiled=True)]
    psum x3 -> x0, blocking collectives: 72.2 us -> none  [the longest x1 38 us: shard_update(): lax.psum(jnp.sum(update * update), ('model', 'data')) / entries]
    pallas_call x0 -> x2, Pallas kernels: none -> 66.9 us  [the longest x1 63.5 us: per_device(): make_reduce_kernel(rows_b, cols, n_model, n_data)]
    unnamed x38 -> x54, local copies, waits for them, and re-layouts: 0.08 us -> 25.4 us
    reduce_sum x14 -> x0, other arithmetic: 15.3 us -> none  [the longest x4 6.88 us: shard_update(): jnp.sum(update * update)]
    add x4 -> x0, other arithmetic: 4.81 us -> none  [shard_update(): return (param + delta, delta, vrow_new, vcol_new)]
  transfers between devices with their start and end apart: 4 -> 0, of which waited for: 4 -> 0; matrix products, arithmetic and copies ran while one was open for 2% -> 0% of each run, Pallas kernels for 0% -> 0%
where the time goes in v1:
time: 98.3 us; the launch traced here: 97.7 us
  Pallas kernels  66.9 us (68%)
  local copies, waits for them, and re-layouts  27.4 us (28%)
  other arithmetic  2.57 us (3%)
    pallas_call x1, Pallas kernels, per_device(): make_reduce_kernel(rows_b, cols, n_model, n_data)  63.5 us
    unnamed x54, local copies, waits for them, and re-layouts  25.4 us
    pallas_call x1, Pallas kernels, per_device(): res = make_apply_kernel(rows_b, cols)(*upd, *params, *vr, *vc, fac)  3.34 us
    pallas_call x2, other arithmetic, per_device(): res = make_apply_kernel(rows_b, cols)(*upd, *params, *vr, *vc, fac)  2.57 us

profile of v1, /device:TPU:0, one launch (start us, length us, event | category | flops | bytes accessed | tf_op | source)
XLA Modules:
  0.0 97.7 jit_solution(16853382987267755322)
XLA Ops:
  0.6 0.7 pad_bitcast_fusion.refs_10_
  1.3 0.7 reshape.84.refs_12_
  2.0 0.7 reshape.85.refs_13_
  2.7 1.1 %copy.34.refs_4_ = f32[128,704]{1,0:T(8,128)S(1)} copy(f32[128,704]{0,1:T(8,128)} %param.17) | data formatting | bytes 720896 | tf_op args[1]
  3.9 0.0 copy-start
  3.9 1.3 %copy.35.refs_5_ = f32[128,704]{1,0:T(8,128)S(1)} copy(f32[128,704]{0,1:T(8,128)} %param.21) | data formatting | bytes 720896 | tf_op args[5]
  5.2 0.0 copy-start.1
  5.2 3.6 %copy.32.refs_0_ = f32[1,1024,704]{2,1,0:T(8,128)} copy(f32[1,1024,704]{1,2,0:T(8,128)} %param.16) | data formatting | bytes 5767168 | tf_op args[0]
  8.8 0.0 copy-start.2
  8.8 0.0 copy-start.3
  8.8 0.0 copy-start.4
  8.8 0.0 copy-start.13
  8.8 0.0 copy-start.14
  8.8 0.0 copy-start.17
  8.8 0.0 copy-start.18
  8.9 0.0 copy-start.19
  8.9 3.6 %copy.33.refs_1_ = f32[1,1024,704]{2,1,0:T(8,128)} copy(f32[1,1024,704]{1,2,0:T(8,128)} %param.20) | data formatting | bytes 5767168 | tf_op args[4]
  12.5 0.0 copy-done
  12.5 0.0 copy-done.1
  12.5 0.0 copy-done.2
  12.5 0.0 copy-done.3
  12.5 0.0 copy-done.4
  12.5 0.0 copy-done.13
  12.5 0.0 copy-done.14
  12.6 0.0 copy-done.17
  12.6 0.0 copy-done.18
  12.6 0.0 copy-done.19
  12.6 63.5 %shard_map.279 = (f32[128,704]{1,0:T(8,128)S(1)}, f32[128,704]{1,0:T(8,128)S(1)}, f32[352,256]{1,0:T(8,128)S(1)}, f32[128,256]{1,0:T(8,128)S(1)}, f32[1,128]{1,0...) custom-call(f32[1,1024,704]{2,1,0:T(8,128)} %copy.32.refs_0_, ...), custom_call_target="tpu_custom_call" | custom-call | tf_op jit(solution)/shard_map/pallas_call | solution.py:390
  76.1 0.0 copy-start.5
  76.1 0.7 copy-done.5
  76.9 0.0 copy-start.6
  76.9 0.7 copy-done.6
  77.6 0.0 copy-start.7
  77.6 0.7 copy-done.7
  78.4 0.0 copy-start.8
  78.4 0.7 copy-done.8
  79.0 0.0 copy-start.9
  79.0 0.6 copy-done.9
  79.6 0.0 copy-start.10
  79.6 0.6 copy-done.10
  80.2 0.0 copy-start.11
  80.2 0.6 copy-done.11
  80.8 0.0 copy-start.12
  80.8 0.6 copy-done.12
  81.3 0.0 copy-start.15
  81.3 0.6 copy-done.15
  81.9 0.0 copy-start.16
  81.9 0.6 copy-done.16
  82.5 0.0 copy-start.20
  82.5 0.6 copy-done.20
  83.1 0.0 copy-start.21
  83.1 0.5 copy-done.21
  83.6 0.0 copy-start.22
  83.6 0.6 copy-done.22
  84.2 3.3 %shard_map.280 = (f32[128,704]{1,0:T(8,128)}, f32[128,704]{1,0:T(8,128)}, f32[352,256]{1,0:T(8,128)}, f32[128,256]{1,0:T(8,128)}, f32[128,704]{1,0:T(8,128)}, /*...) custom-call(f32[128,704]{1,0:T(8,128)} %copy-done.5, ...), custom_call_target="tpu_custom_call" | custom-call | tf_op jit(solution)/shard_map/pallas_call | solution.py:392
  87.5 1.9 %copy.38 = f32[128,704]{0,1:T(8,128)} copy(f32[128,704]{1,0:T(8,128)} %get-tuple-element.74) | data formatting | bytes 720896
  89.4 1.3 %reduce = f32[704]{0:T(1024)} reduce(f32[1,704]{1,0:T(1,128)} %get-tuple-element.61, f32[]{:T(128)} %constant.9), dimensions={0}, to_apply=%get-tuple-element.61.reduce_sub_computation | reduce | bytes 5636 | tf_op jit(solution)/shard_map/pallas_call | solution.py:392
  90.7 1.3 %reduce.1 = f32[704]{0:T(1024)} reduce(f32[1,704]{1,0:T(1,128)} %get-tuple-element.65, f32[]{:T(128)} %constant.9), dimensions={0}, to_apply=%get-tuple-element.65.reduce_sub_computation | reduce | bytes 5636 | tf_op jit(solution)/shard_map/pallas_call | solution.py:392
  92.0 1.9 %copy.39 = f32[128,704]{0,1:T(8,128)} copy(f32[128,704]{1,0:T(8,128)} %get-tuple-element.75) | data formatting | bytes 720896
  93.9 1.9 %copy.40 = f32[128,704]{0,1:T(8,128)} copy(f32[128,704]{1,0:T(8,128)} %get-tuple-element.78) | data formatting | bytes 720896
  95.8 1.9 %copy.41 = f32[128,704]{0,1:T(8,128)} copy(f32[128,704]{1,0:T(8,128)} %get-tuple-element.79) | data formatting | bytes 720896
Async XLA Ops:
  3.9 8.6 %copy-start = (f32[128,704]{1,0:T(8,128)}, f32[128,704]{1,0:T(8,128)S(1)}, u32[]{:S(2)}) copy-start(f32[128,704]{1,0:T(8,128)S(1)} %copy.34.refs_4_) | copy-start | bytes 1081348
  5.2 7.3 %copy-start.1 = (f32[128,704]{1,0:T(8,128)}, f32[128,704]{1,0:T(8,128)S(1)}, u32[]{:S(2)}) copy-start(f32[128,704]{1,0:T(8,128)S(1)} %copy.35.refs_5_) | copy-start | bytes 1081348
  8.8 3.7 %copy-start.2 = (f32[352,256]{1,0:T(8,128)S(1)}, f32[352,256]{1,0:T(8,128)}, u32[]{:S(2)}) copy-start(f32[352,256]{1,0:T(8,128)} %refs_6_.3) | copy-start | bytes 1081348
  8.8 3.7 %copy-start.3 = (f32[1,1024,256]{2,1,0:T(8,128)S(1)}, f32[1,1024,256]{2,1,0:T(8,128)}, u32[]{:S(2)}) copy-start(f32[1,1024,256]{2,1,0:T(8,128)} %refs_3_.1) | copy-start | bytes 3145732
  8.8 3.7 %copy-start.4 = (f32[128,256]{1,0:T(8,128)S(1)}, f32[128,256]{1,0:T(8,128)}, u32[]{:S(2)}) copy-start(f32[128,256]{1,0:T(8,128)} %refs_7_.3) | copy-start | bytes 393220
  8.8 3.7 %copy-start.13 = (f32[256]{0:T(256)S(1)}, f32[256]{0:T(256)}, u32[]{:S(2)}) copy-start(f32[256]{0:T(256)} %param.27) | copy-start | bytes 3076
  8.8 3.7 %copy-start.14 = (f32[256]{0:T(256)S(1)}, f32[256]{0:T(256)}, u32[]{:S(2)}) copy-start(f32[256]{0:T(256)} %param.31) | copy-start | bytes 3076
  8.8 3.7 %copy-start.17 = (f32[128]{0:T(128)S(1)}, f32[128]{0:T(128)}, u32[]{:S(2)}) copy-start(f32[128]{0:T(128)} %param.18) | copy-start | bytes 1540
  8.8 3.7 %copy-start.18 = (f32[128]{0:T(128)S(1)}, f32[128]{0:T(128)}, u32[]{:S(2)}) copy-start(f32[128]{0:T(128)} %param.22) | copy-start | bytes 1540
  8.9 3.7 %copy-start.19 = (f32[128]{0:T(128)S(1)}, f32[128]{0:T(128)}, u32[]{:S(2)}) copy-start(f32[128]{0:T(128)} %param.30) | copy-start | bytes 1540
  76.1 0.7 copy-start.5
  76.9 0.7 copy-start.6
  77.6 0.7 copy-start.7
  78.4 0.7 copy-start.8
  79.0 0.6 copy-start.9
  79.6 0.6 copy-start.10
  80.2 0.6 copy-start.11
  80.8 0.6 copy-start.12
  81.3 0.6 copy-start.15
  81.9 0.6 copy-start.16
  82.5 0.6 copy-start.20
  83.1 0.5 copy-start.21
  83.6 0.6 copy-start.22

commit v2 on v1

v2 whole, which is shorter than its diff:
```python
import jax
import jax.numpy as jnp
from jax import lax
from jax.experimental import pallas as pl
from jax.experimental.pallas import tpu as pltpu
from jax.sharding import PartitionSpec as P

OPT_STEP = 3
BETA = 1.0 - OPT_STEP ** -0.8
LR_REL = min(0.01, OPT_STEP ** -0.5)
NM = 4
OWN, NX, NY, ND = 0, 1, 2, 3
STEP_ROWS = (88, 88, 88, 64)
MESH_ID = pl.DeviceIdType.MESH


def layout_of(rows_b, cols, n_model, n_data):
    mats = []
    for r, c in zip(rows_b, cols):
        flip = c % 128 != 0
        n0, n1 = (c, r) if flip else (r, c)
        mats.append(dict(flip=flip, n0=n0, n1=n1, half=n0 // 2, groups=n0 // 8, tiles=-(-n0 // 128), lanes=n1 // 128,
                         rows_b=r, rows_t=r * n_data, cols_t=c * n_model,
                         size=float(r * n_data * c * n_model)))
    return mats


def make_reduce_kernel(rows_b, cols, n_model, n_data):
    mats = layout_of(rows_b, cols, n_model, n_data)

    def kernel(*refs):
        grads = refs[0:4]
        params = refs[4:8]
        vrows = refs[8:12]
        vcols = refs[12:16]
        upd = refs[16:20]
        wbuf = refs[20:24]
        stats = refs[24]
        sc = list(refs[25:])
        take = lambda n: [sc.pop(0) for _ in range(n)]
        loc, rec, fx, fy, vrbuf, vcbuf = (take(4) for _ in range(6))
        rmsg, rrx, cmsg, crx, bmsg, brx, vrc, vcc, stage = take(9)
        (ld_sem, dd_s, dd_r, x_s, x_r, y_s, y_r, in_sem,
         ra_s, ra_r, ca_s, ca_r, b_s, b_r) = take(14)
        greet = take(1)[0]

        z = lax.axis_index('model')
        d = lax.axis_index('data')
        core = lax.rem(d, 2)
        xx = lax.rem(d // 2, 2)
        yy = d // 4
        sib = d + 1 - 2 * core
        dx = d + 2 - 4 * xx
        dy = d + 4 - 8 * yy
        dd = dx + 4 - 8 * yy
        owner = {OWN: d, NX: dx, NY: dy, ND: dd}
        sib_step = 1 - 2 * core

        lane = lax.broadcasted_iota(jnp.int32, (8, 128), 1)
        sub = lax.broadcasted_iota(jnp.int32, (8, 128), 0)

        def remote(src, dst, ssem, rsem, data=None, model=None):
            return pltpu.make_async_remote_copy(
                src_ref=src, dst_ref=dst, send_sem=ssem, recv_sem=rsem,
                device_id=(z if model is None else model, d if data is None else data),
                device_id_type=MESH_ID)

        def signal(sem, data=None, model=None):
            pl.semaphore_signal(
                sem, inc=1,
                device_id=(z if model is None else model, d if data is None else data),
                device_id_type=MESH_ID)

        order = []
        for m in range(NM):
            order += [(m, ND, 0), (m, ND, 1), (m, NX, 0), (m, NY, 1)]
        for m in range(NM):
            order += [(m, NY, 0), (m, NX, 1)]
        for m in range(NM):
            order += [(m, OWN, 0), (m, OWN, 1)]

        def slot(m, j, h):
            return (m * 4 + j) * 2 + h

        def block(m, who, h):
            q = mats[m]
            if q['flip']:
                cut = pl.ds(pl.multiple_of(who * q['n1'], 128), q['n1'])
                return grads[m].at[0, pl.ds(h * q['half'], q['half']), cut]
            return grads[m].at[0, pl.ds(pl.multiple_of(who * q['n0'] + h * q['half'], 8), q['half']), :]

        loads = {}
        for m, j, h in order:
            loads[m, j, h] = pltpu.make_async_copy(block(m, owner[j], h), loc[m].at[j, h], ld_sem.at[slot(m, j, h)])
            loads[m, j, h].start()
        small = []
        for m in range(NM):
            small.append(pltpu.make_async_copy(params[m], wbuf[m], in_sem.at[m]))
            small.append(pltpu.make_async_copy(vrows[m], vrbuf[m], in_sem.at[4 + m]))
            small.append(pltpu.make_async_copy(vcols[m], vcbuf[m], in_sem.at[8 + m]))
        for cp in small:
            cp.start()

        barrier = pltpu.get_barrier_semaphore()
        for peer in (sib, dx, dy):
            signal(barrier, data=peer)
        up_ok = z < n_model - 1
        down_ok = z > 0

        def signal_z(sem):
            @pl.when(up_ok)
            def _():
                signal(sem, model=z + 1)

            @pl.when(down_ok)
            def _():
                signal(sem, model=z - 1)

        n_z = jnp.where(up_ok, 1, 0) + jnp.where(down_ok, 1, 0)
        signal_z(barrier)
        pl.semaphore_wait(barrier, 3 + n_z)

        dsend = {}
        for m, j, h in order:
            k = slot(m, j, h)
            dsend[m, j, h] = remote(block(m, owner[j] + sib_step, h), rec[m].at[j, h], dd_s.at[k], dd_r.at[k], data=sib)
            dsend[m, j, h].start()

        def pair_sum(m, j, h, extra=None):
            loads[m, j, h].wait()
            dsend[m, j, h].wait_recv()
            total = loc[m][j, h] + rec[m][j, h]
            if extra is not None:
                total = total + extra
            loc[m][j, h] = total

        xsend, ysend = {}, {}
        for m in range(NM):
            for i, (j, h) in enumerate(((ND, 0), (NX, 0), (NX, 1))):
                xsend[m, i] = remote(loc[m].at[j, h], fx[m].at[i], x_s.at[3 * m + i], x_r.at[3 * m + i], data=dx)
            for i, (j, h) in enumerate(((ND, 1), (NY, 0), (NY, 1))):
                ysend[m, i] = remote(loc[m].at[j, h], fy[m].at[i], y_s.at[3 * m + i], y_r.at[3 * m + i], data=dy)

        for m in range(NM):
            pair_sum(m, ND, 0)
            xsend[m, 0].start()
            pair_sum(m, ND, 1)
            ysend[m, 0].start()
            pair_sum(m, NX, 0)
            xsend[m, 1].start()
            pair_sum(m, NY, 1)
            ysend[m, 2].start()

        for cp in small:
            cp.wait()

        def rows_of(buf, n, i):
            stage[i] = jnp.zeros((8, 128), jnp.float32)
            for t in range(-(-n // 128)):
                n_t = min(128, n - 128 * t)
                stage[i, t:t + 1, 0:n_t] = buf[pl.ds(128 * t, n_t)].reshape(1, n_t)

        def to_compact(i, n):
            acc = jnp.zeros((8, 128), jnp.float32)
            for t in range(-(-n // 128)):
                row = jnp.broadcast_to(stage[i, t:t + 1, :], (8, 128))
                for g in range(min(128, n - 128 * t) // 8):
                    col = jnp.sum(jnp.where(lane == 8 * g + sub, row, 0.0), axis=1, keepdims=True)
                    acc = jnp.where(lane == 16 * t + g, col, acc)
            return acc

        bv = jnp.zeros((8, 128), jnp.float32)
        for m in range(NM):
            q = mats[m]
            w = wbuf[m][...]
            part = jnp.sum(w * w, axis=(0, 1), keepdims=True) * (1.0 / q['size'])
            bv = jnp.where((sub == 2) & (lane == m), part, bv)
            rows_of(vrbuf[m], q['rows_b'], 2 * m)
            rows_of(vcbuf[m], cols[m], 2 * m + 1)
            if q['flip']:
                vrc[m] = stage[2 * m]
                vcc[m] = to_compact(2 * m + 1, q['n0'])
            else:
                vrc[m] = to_compact(2 * m, q['n0'])
                vcc[m] = stage[2 * m + 1]
            rmsg[m] = jnp.zeros((8, 128), jnp.float32)
            cmsg[m] = jnp.zeros((8, 128), jnp.float32)
        bmsg[...] = bv

        signal(greet.at[0], data=sib)
        pl.semaphore_wait(greet.at[0], 1)
        signal(greet.at[1], data=dx)
        pl.semaphore_wait(greet.at[1], 1)
        signal(greet.at[2], data=dy)
        pl.semaphore_wait(greet.at[2], 1)
        signal_z(greet.at[3])
        pl.semaphore_wait(greet.at[3], n_z)
        signal_z(greet.at[4])
        pl.semaphore_wait(greet.at[4], n_z)

        for m in range(NM):
            xsend[m, 0].wait_recv()
            pair_sum(m, NY, 0, fx[m][0])
            ysend[m, 1].start()
            ysend[m, 0].wait_recv()
            pair_sum(m, NX, 1, fy[m][0])
            xsend[m, 2].start()

        rsend, csend = {}, {}
        for m in range(NM):
            for k in range(1, n_model):
                i = m * (n_model - 1) + k - 1
                rsend[m, k] = remote(rmsg.at[m], rrx.at[i], ra_s.at[i], ra_r.at[i],
                                     model=lax.rem(z + k, n_model))
            for k in range(1, n_data):
                i = m * (n_data - 1) + k - 1
                csend[m, k] = remote(cmsg.at[m], crx.at[i], ca_s.at[i], ca_r.at[i],
                                     data=lax.rem(d + k, n_data))

        for m in range(NM):
            q = mats[m]
            step = STEP_ROWS[m]
            acc1 = jnp.zeros((8, q['n1']), jnp.float32)
            acc0 = jnp.zeros((8, 128), jnp.float32)
            for h in range(2):
                loads[m, OWN, h].wait()
                dsend[m, OWN, h].wait_recv()
                xsend[m, 1 + h].wait_recv()
                ysend[m, 1 + h].wait_recv()

                def body(it, carry, m=m, h=h, step=step, half=q['half']):
                    acc1, acc0 = carry
                    r0 = pl.multiple_of(it * step, 8)
                    rows = pl.ds(r0, step)
                    total = (loc[m][OWN, h, rows, :] + rec[m][OWN, h, rows, :]
                             + fx[m][1 + h, rows, :] + fy[m][1 + h, rows, :])
                    upd[m][pl.ds(pl.multiple_of(h * half + r0, 8), step), :] = total
                    sq = total * total + 1e-30
                    for g in range(step // 8):
                        part = sq[8 * g:8 * g + 8, :]
                        acc1 = acc1 + part
                        rsum = jnp.sum(part, axis=1, keepdims=True)
                        acc0 = jnp.where(lane == (h * half + it * step) // 8 + g, rsum, acc0)
                    return acc1, acc0

                acc1, acc0 = lax.fori_loop(0, q['half'] // step, body, (acc1, acc0))
            sum1 = jnp.sum(acc1, axis=0, keepdims=True)
            msg0, msg1 = (cmsg, rmsg) if q['flip'] else (rmsg, cmsg)
            msg0[m] = acc0
            for k in range(q['lanes']):
                msg1[m, k:k + 1, :] = sum1[:, 128 * k:128 * k + 128]
            for k in range(1, n_model):
                rsend[m, k].start()
            for k in range(n_data - 1, 0, -1):
                csend[m, k].start()

        bv = bmsg[...]
        locrow = jnp.ones((8, 128), jnp.float32)
        for m in range(NM):
            q = mats[m]
            rtot = rmsg[m]
            for k in range(1, n_model):
                rsend[m, k].wait_recv()
                rtot = rtot + rrx[m * (n_model - 1) + k - 1]
            ctot = cmsg[m]
            for k in range(1, n_data):
                csend[m, k].wait_recv()
                ctot = ctot + crx[m * (n_data - 1) + k - 1]
            vr = BETA * vrc[m] + (1.0 - BETA) * (rtot * (1.0 / q['cols_t']))
            vc = BETA * vcc[m] + (1.0 - BETA) * (ctot * (1.0 / q['rows_t']))
            ok0 = lane < q['groups']
            ok1 = sub < q['lanes']
            okr, okc = (ok1, ok0) if q['flip'] else (ok0, ok1)
            vr_sum = jnp.sum(jnp.where(okr, vr, 0.0), axis=(0, 1), keepdims=True)
            mloc = vr_sum * (1.0 / q['rows_b'])
            rfac = lax.rsqrt(jnp.where(okr, vr / mloc, 1.0))
            cfac = lax.rsqrt(jnp.where(okc, vc, 1.0))
            fac0, fac1 = (cfac, rfac) if q['flip'] else (rfac, cfac)
            if q['flip']:
                vcc[m] = vc
                stats[1 + 2 * m] = vr
            else:
                vcc[m] = vr
                stats[1 + 2 * m] = vc
            f1 = jnp.concatenate([jnp.broadcast_to(fac1[k:k + 1, :], (8, 128)) for k in range(q['lanes'])], axis=1)
            step = STEP_ROWS[m]

            def tbody(it, tacc, m=m, step=step, f1=f1, fac0=fac0):
                for g in range(step // 8):
                    r0 = pl.multiple_of(it * step + 8 * g, 8)
                    f0 = jnp.sum(jnp.where(lane == it * (step // 8) + g, fac0, 0.0), axis=1, keepdims=True)
                    u = upd[m][pl.ds(r0, 8), :] * f0 * f1
                    upd[m][pl.ds(r0, 8), :] = u
                    tacc = tacc + u * u
                return tacc

            tacc = lax.fori_loop(0, q['n0'] // step, tbody, jnp.zeros((8, q['n1']), jnp.float32))
            t_m = jnp.sum(tacc, axis=(0, 1), keepdims=True) * (1.0 / q['size'])
            bv = jnp.where((sub == 0) & (lane == m), t_m / mloc, bv)
            bv = jnp.where((sub == 1) & (lane == m), vr_sum * (1.0 / (q['rows_t'] * n_model)), bv)
            locrow = jnp.where(lane == m, mloc, locrow)

        bmsg[...] = bv
        bsend = []
        for kz in range(n_model):
            for kd in range(n_data):
                if kz == 0 and kd == 0:
                    continue
                i = kz * n_data + kd - 1
                bsend.append(remote(bmsg, brx.at[i], b_s.at[i], b_r.at[i],
                                    data=lax.rem(d + kd, n_data), model=lax.rem(z + kz, n_model)))
        for cp in reversed(bsend):
            cp.start()

        for m in range(NM):
            q = mats[m]
            v = vcc[m]
            out = jnp.zeros((8, 128), jnp.float32)
            for t in range(q['tiles']):
                acc = jnp.zeros((8, 128), jnp.float32)
                for g in range(min(128, q['n0'] - 128 * t) // 8):
                    col = jnp.sum(jnp.where(lane == 16 * t + g, v, 0.0), axis=1, keepdims=True)
                    acc = jnp.where(lane == 8 * g + sub, col, acc)
                out = jnp.where(sub == t, jnp.sum(acc, axis=0, keepdims=True), out)
            stats[2 + 2 * m] = out

        for cp in bsend:
            cp.wait_recv()
        tot = bmsg[...]
        for i in range(n_model * n_data - 1):
            tot = tot + brx[i]
        mean_vr = tot[1:2, :]
        u_rms = jnp.sqrt(mean_vr * tot[0:1, :])
        w_rms = jnp.sqrt(tot[2:3, :])
        fac = -(LR_REL * jnp.maximum(1e-3, w_rms)) * (jnp.sqrt(mean_vr) * lax.rsqrt(locrow[0:1, :]))
        stats[0] = jnp.broadcast_to(fac / jnp.maximum(1.0, u_rms), (8, 128))

        for key in dsend:
            dsend[key].wait_send()
        for group in (xsend, ysend, rsend, csend):
            for key in group:
                group[key].wait_send()
        for cp in bsend:
            cp.wait_send()

    f32 = jnp.float32
    n_row_msgs = NM * (n_model - 1)
    n_col_msgs = NM * (n_data - 1)
    n_b = n_model * n_data - 1
    dma = pltpu.SemaphoreType.DMA
    vm = pltpu.VMEM
    scratch = []
    scratch += [vm((4, 2, q['half'], q['n1']), f32) for q in mats]
    scratch += [vm((4, 2, q['half'], q['n1']), f32) for q in mats]
    scratch += [vm((3, q['half'], q['n1']), f32) for q in mats]
    scratch += [vm((3, q['half'], q['n1']), f32) for q in mats]
    scratch += [vm((r,), f32) for r in rows_b]
    scratch += [vm((c,), f32) for c in cols]
    tile = lambda *lead: vm((*lead, 8, 128), f32)
    scratch += [tile(NM), tile(n_row_msgs), tile(NM), tile(n_col_msgs), tile(), tile(n_b),
                tile(NM), tile(NM), tile(2 * NM)]
    scratch += [dma((32,)), dma((32,)), dma((32,)), dma((12,)), dma((12,)), dma((12,)), dma((12,)), dma((12,)),
                dma((n_row_msgs,)), dma((n_row_msgs,)), dma((n_col_msgs,)), dma((n_col_msgs,)),
                dma((n_b,)), dma((n_b,))]
    scratch += [pltpu.SemaphoreType.REGULAR((5,))]
    blocks = [jax.ShapeDtypeStruct((q['n0'], q['n1']), f32) for q in mats]
    out_shape = blocks + blocks + [jax.ShapeDtypeStruct((1 + 2 * NM, 8, 128), f32)]
    vmem = pl.BlockSpec(memory_space=pltpu.VMEM)
    hbm = pl.BlockSpec(memory_space=pltpu.HBM)
    return pl.pallas_call(
        kernel, out_shape=out_shape, in_specs=[hbm] * 16, out_specs=[vmem] * len(out_shape),
        scratch_shapes=scratch,
        compiler_params=pltpu.CompilerParams(collective_id=0, has_side_effects=True,
                                             vmem_limit_bytes=28 * 1024 * 1024))


def make_apply_kernel(rows_b, cols, n_model, n_data):
    mats = layout_of(rows_b, cols, n_model, n_data)

    def kernel(*refs):
        upd, params, stats = refs[0:4], refs[4:8], refs[8]
        new, delta, vrow_out, vcol_out = refs[9:13], refs[13:17], refs[17:21], refs[21:25]
        bufs = refs[25:33]
        sem = refs[33]
        copies = []
        for m in range(NM):
            fac = stats[0, 0:1, m:m + 1]
            step = fac * upd[m][...]
            bufs[4 + m][...] = step
            bufs[m][...] = params[m][...] + step
            for i, out in ((m, new[m]), (4 + m, delta[m])):
                copies.append(pltpu.make_async_copy(bufs[i], out, sem.at[i]))
                copies[-1].start()
        for m in range(NM):
            q = mats[m]
            out1, out0 = (vrow_out[m], vcol_out[m]) if q['flip'] else (vcol_out[m], vrow_out[m])
            for k in range(q['lanes']):
                out1[pl.ds(128 * k, 128)] = stats[1 + 2 * m, k:k + 1, :].reshape(128)
            for t in range(q['tiles']):
                n_t = min(128, q['n0'] - 128 * t)
                out0[pl.ds(128 * t, n_t)] = stats[2 + 2 * m, t:t + 1, 0:n_t].reshape(n_t)
        for cp in copies:
            cp.wait()

    f32 = jnp.float32
    vmem = pl.BlockSpec(memory_space=pltpu.VMEM)
    hbm = pl.BlockSpec(memory_space=pltpu.HBM)
    blocks = [jax.ShapeDtypeStruct((q['n0'], q['n1']), f32) for q in mats]
    out_shape = (blocks + blocks + [jax.ShapeDtypeStruct((r,), f32) for r in rows_b]
                 + [jax.ShapeDtypeStruct((c,), f32) for c in cols])
    return pl.pallas_call(
        kernel, out_shape=out_shape, in_specs=[vmem] * 9, out_specs=[hbm] * 8 + [vmem] * 8,
        scratch_shapes=[pltpu.VMEM((q['n0'], q['n1']), f32) for q in mats] * 2 + [pltpu.SemaphoreType.DMA((8,))],
        compiler_params=pltpu.CompilerParams(vmem_limit_bytes=6 * 1024 * 1024))


def solution(mesh):
    n_data = mesh.shape['data']
    n_model = mesh.shape['model']
    mat_spec = P('data', 'model')
    in_specs = (P('data', None, 'model'), mat_spec, P('data'), P('model')) * NM
    out_specs = (mat_spec, mat_spec, P('data'), P('model')) * NM

    def per_device(*arrays):
        grads, params = arrays[0::4], arrays[1::4]
        rows_b = [p.shape[0] for p in params]
        cols = [p.shape[1] for p in params]
        mats = layout_of(rows_b, cols, n_model, n_data)
        view = lambda i, a: jnp.swapaxes(a, -1, -2) if mats[i]['flip'] else a
        grads = [view(i, g) for i, g in enumerate(grads)]
        params = [view(i, p) for i, p in enumerate(params)]
        pin = lambda a: pltpu.with_memory_space_constraint(a, pltpu.HBM)
        outs = make_reduce_kernel(rows_b, cols, n_model, n_data)(
            *map(pin, grads), *map(pin, params), *map(pin, arrays[2::4]), *map(pin, arrays[3::4]))
        res = make_apply_kernel(rows_b, cols, n_model, n_data)(*outs)
        flat = []
        for m in range(NM):
            flat += [view(m, res[m]), view(m, res[4 + m]), res[8 + m], res[12 + m]]
        return tuple(flat)

    return jax.shard_map(per_device, mesh=mesh, in_specs=in_specs, out_specs=out_specs, check_vma=False)
```

time: 98.3 us -> 63.4 us (0.64)
  local copies, waits for them, and re-layouts: 27.4 us -> 0 us
  Pallas kernels: 66.9 us -> 62.6 us
  other arithmetic: 2.57 us -> 0 us
    unnamed x54 -> x0, local copies, waits for them, and re-layouts: 25.4 us -> none
    pallas_call x1, Pallas kernels: 63.5 us -> 60.4 us  [per_device(): make_reduce_kernel(rows_b, cols, n_model, n_data)]
    pallas_call x2 -> x0, other arithmetic: 2.57 us -> none  [per_device(): res = make_apply_kernel(rows_b, cols)(*upd, *params, *vr, *vc, fac)]
    reshape x3 -> x0, local copies, waits for them, and re-layouts: 2.06 us -> none  [the longest x2 1.38 us: per_device(): vcols = [v.reshape(1, -1) for v in arrays[3::4]]]
    pallas_call x1, Pallas kernels: 3.34 us -> 2.19 us  [per_device(): res = make_apply_kernel(rows_b, cols, n_model, n_data)(*outs)]
where the time goes in v2:
time: 63.4 us; the launch traced here: 63.3 us
  Pallas kernels  62.6 us (99%)
  between operations  0.66 us (1%)
    pallas_call x1, Pallas kernels, per_device(): make_reduce_kernel(rows_b, cols, n_model, n_data)  60.4 us
    pallas_call x1, Pallas kernels, per_device(): res = make_apply_kernel(rows_b, cols, n_model, n_data)(*outs)  2.19 us

profile of v2, /device:TPU:0, one launch (start us, length us, event | category | flops | bytes accessed | tf_op | source)
XLA Modules:
  0.0 63.3 jit_solution(1928960716037985877)
XLA Ops:
  0.7 60.4 %shard_map.279 = (f32[704,128]{1,0:T(8,128)S(1)}, f32[704,128]{1,0:T(8,128)S(1)}, f32[352,256]{1,0:T(8,128)S(1)}, f32[128,256]{1,0:T(8,128)S(1)}, f32[704,128]{1...) custom-call(f32[1,704,1024]{2,1,0:T(8,128)} %bitcast.8, ...), custom_call_target="tpu_custom_call" | custom-call | tf_op jit(solution)/shard_map/pallas_call | solution.py:433
  61.1 2.2 %shard_map.280 = (f32[704,128]{1,0:T(8,128)}, f32[704,128]{1,0:T(8,128)}, f32[352,256]{1,0:T(8,128)}, f32[128,256]{1,0:T(8,128)}, f32[704,128]{1,0:T(8,128)}, /*...) custom-call(f32[704,128]{1,0:T(8,128)S(1)} %get-tuple-element.41.ref, ...), custom_call_target="tpu_custom_call" | custom-call | tf_op jit(solution)/shard_map/pallas_call | solution.py:435

commit v3 on v0

v3 whole, which is shorter than its diff:
```python
import jax
import jax.numpy as jnp
from jax import lax
from jax.experimental import pallas as pl
from jax.experimental.pallas import tpu as pltpu
from jax.sharding import PartitionSpec as P

OPT_STEP = 3
BETA = 1.0 - OPT_STEP ** -0.8
LR_REL = min(0.01, OPT_STEP ** -0.5)
NM = 4
OWN, NX, NY, ND = 0, 1, 2, 3
FIRST_ROWS = 88
MESH_ID = pl.DeviceIdType.MESH


def layout_of(rows_b, cols, n_model, n_data):
    mats = []
    for r, c in zip(rows_b, cols):
        flip = c % 128 != 0
        n0, n1 = (c, r) if flip else (r, c)
        mats.append(dict(flip=flip, n0=n0, n1=n1, half=n0 // 2, groups=n0 // 8, tiles=-(-n0 // 128), lanes=n1 // 128,
                         rows_b=r, rows_t=r * n_data, cols_t=c * n_model,
                         size=float(r * n_data * c * n_model)))
    return mats


def make_reduce_kernel(rows_b, cols, n_model, n_data):
    mats = layout_of(rows_b, cols, n_model, n_data)
    halves = [q['half'] for q in mats]
    first = []
    for lo, hi in ((0, FIRST_ROWS), (FIRST_ROWS, halves[0])):
        first += [(0, ND, lo, hi - lo), (0, ND, halves[0] + lo, hi - lo)]
    whole = {(m, j): (m, j, 0, mats[m]['n0']) for m in range(NM) for j in (OWN, NX, NY, ND) if (m, j) != (0, ND)}
    fetches = first + list(whole.values())
    index = {f: i for i, f in enumerate(fetches)}
    ld_slot = {f: i for i, f in enumerate(first)}
    for m in range(NM):
        for i, j in enumerate((ND, NX, NY)):
            if (m, j) in whole:
                ld_slot[whole[m, j]] = {0: 3 + i, 1: 6 + i, 2: (0, 4, 5)[i], 3: 6 + i}[m]
        ld_slot[whole[m, OWN]] = 9 + m

    def kernel(*refs):
        grads = refs[0:4]
        params = refs[4:8]
        vrows = refs[8:12]
        vcols = refs[12:16]
        upd = refs[16:20]
        wbuf = refs[20:24]
        stats = refs[24]
        sc = list(refs[25:])
        take = lambda n: [sc.pop(0) for _ in range(n)]
        loc, rec, fxy, vrbuf, vcbuf = (take(4) for _ in range(5))
        stg, rmsg, rrx, cmsg, crx, csib, brx, vrc, vcc, stage = take(10)
        ld_sem, dd_s, dd_r, l_s, l_r, in_sem, a_s, ra_r, ca_r, cs_r, b_s, b_r, greet = take(13)

        z = lax.axis_index('model')
        d = lax.axis_index('data')
        core = lax.rem(d, 2)
        xx = lax.rem(d // 2, 2)
        yy = d // 4
        sib_step = 1 - 2 * core
        sib = d + sib_step
        dx = d + 2 - 4 * xx
        dy = d + 4 - 8 * yy
        dd = dx + 4 - 8 * yy
        owner = {OWN: d, NX: dx, NY: dy, ND: dd}

        def remote(src, dst, ssem, rsem, data=None, model=None):
            return pltpu.make_async_remote_copy(
                src_ref=src, dst_ref=dst, send_sem=ssem, recv_sem=rsem,
                device_id=(z if model is None else model, d if data is None else data),
                device_id_type=MESH_ID)

        def signal(sem, data=None, model=None):
            pl.semaphore_signal(
                sem, inc=1,
                device_id=(z if model is None else model, d if data is None else data),
                device_id_type=MESH_ID)

        def wait_bytes(ref, sem):
            pltpu.make_async_copy(ref, ref, sem).wait()

        barrier = pltpu.get_barrier_semaphore()
        for peer in (sib, dx, dy):
            signal(barrier, data=peer)
        up_ok = z < n_model - 1
        down_ok = z > 0

        def signal_z(sem):
            @pl.when(up_ok)
            def _():
                signal(sem, model=z + 1)

            @pl.when(down_ok)
            def _():
                signal(sem, model=z - 1)

        n_z = jnp.where(up_ok, 1, 0) + jnp.where(down_ok, 1, 0)
        signal_z(barrier)

        def block(who, f):
            m, j, r0, n = f
            q = mats[m]
            if q['flip']:
                cut = pl.ds(pl.multiple_of(who * q['n1'], 128), q['n1'])
                return grads[m].at[0, pl.ds(r0, n), cut]
            return grads[m].at[0, pl.ds(pl.multiple_of(who * q['n0'] + r0, 8), n), :]

        loads, dsend, stage_in = {}, {}, {}
        for f in fetches:
            m, j, r0, n = f
            part = (m, pl.ds(r0, n))
            loads[f] = pltpu.make_async_copy(block(owner[j], f), loc[m].at[j, pl.ds(r0, n), :], ld_sem.at[ld_slot[f]])
            source = block(owner[j] + sib_step, f)
            if f in first:
                held = stg.at[pl.ds(r0, n), :]
                stage_in[f] = pltpu.make_async_copy(source, held, ld_sem.at[9 + first.index(f)])
                source = held
            dsend[f] = remote(source, rec[m].at[j, pl.ds(r0, n), :], dd_s.at[m], dd_r.at[index[f]], data=sib)

        def fetch(pieces):
            for f in pieces:
                dsend[f].start()
                loads[f].start()

        def fetch_done(f):
            loads[f].wait()
            dsend[f].wait_recv()

        def link_send(m, j, r0, n):
            h, off = (0, r0) if r0 < halves[m] else (1, r0 - halves[m])
            along_x = (j == ND and h == 0) or j == NX
            slot = (0 if along_x else 3) + (0 if j == ND else 1 + h)
            return remote(loc[m].at[j, pl.ds(r0, n), :], fxy[m].at[slot, pl.ds(off, n), :],
                          l_s.at[m], l_r.at[6 * m + slot], data=dx if along_x else dy)

        def arrived(m, slot):
            wait_bytes(fxy[m].at[slot], l_r.at[6 * m + slot])

        def pair_sum(m, j, r0, n, relay=None):
            total = loc[m][j, r0:r0 + n, :] + rec[m][j, r0:r0 + n, :]
            if relay is not None:
                total = total + fxy[m][relay]
            loc[m][j, r0:r0 + n, :] = total
            link_send(m, j, r0, n).start()

        def send_raw(m):
            n = halves[m]
            fetch_done(whole[m, ND])
            pair_sum(m, ND, 0, n)
            pair_sum(m, ND, n, n)
            send_near(m)

        def send_near(m):
            n = halves[m]
            fetch_done(whole[m, NX])
            pair_sum(m, NX, 0, n)
            fetch_done(whole[m, NY])
            pair_sum(m, NY, n, n)

        def send_acc(m):
            n = halves[m]
            arrived(m, 0)
            pair_sum(m, NY, 0, n, 0)
            arrived(m, 3)
            pair_sum(m, NX, n, n, 3)

        for f in first:
            stage_in[f].start()
        for f in first:
            loads[f].start()
        pl.semaphore_wait(barrier, 3 + n_z)
        for f in first:
            stage_in[f].wait()
            dsend[f].start()
        fetch([whole[0, NX], whole[0, NY]])
        for f in first[0:2]:
            fetch_done(f)
            pair_sum(*f)
        fetch([whole[1, ND], whole[1, NX], whole[1, NY]])
        for f in first[2:4]:
            fetch_done(f)
            pair_sum(*f)
        send_near(0)
        fetch([whole[2, ND], whole[2, NX], whole[2, NY]])
        send_raw(1)
        fetch([whole[3, ND], whole[3, NX], whole[3, NY]])
        fetch([whole[m, OWN] for m in range(NM)])
        small = []
        for m in range(NM):
            small.append(pltpu.make_async_copy(params[m], wbuf[m], in_sem.at[m]))
            small.append(pltpu.make_async_copy(vrows[m], vrbuf[m], in_sem.at[4 + m]))
            small.append(pltpu.make_async_copy(vcols[m], vcbuf[m], in_sem.at[8 + m]))
        for cp in small:
            cp.start()

        lane = lax.broadcasted_iota(jnp.int32, (8, 128), 1)
        sub = lax.broadcasted_iota(jnp.int32, (8, 128), 0)
        lane1 = lax.broadcasted_iota(jnp.int32, (1, 128), 1)

        def group_mask(g):
            shape = (g, 8, 128)
            return lax.broadcasted_iota(jnp.int32, shape, 2) == lax.broadcasted_iota(jnp.int32, shape, 0)

        def compact(values):
            return jnp.sum(jnp.where(group_mask(values.shape[0]), values, 0.0), axis=0)

        def expand(vec, g):
            return jnp.sum(jnp.where(group_mask(g), vec[None], 0.0), axis=2, keepdims=True)

        def rows_of(buf, n, i):
            stage[i] = jnp.zeros((8, 128), jnp.float32)
            for t in range(-(-n // 128)):
                n_t = min(128, n - 128 * t)
                stage[i, t:t + 1, 0:n_t] = buf[pl.ds(128 * t, n_t)].reshape(1, n_t)

        def to_compact(i, n):
            out = jnp.zeros((8, 128), jnp.float32)
            for t in range(-(-n // 128)):
                row = jnp.broadcast_to(stage[i, t:t + 1, :], (8, 128))
                for g in range(min(128, n - 128 * t) // 8):
                    col = jnp.sum(jnp.where(lane == 8 * g + sub, row, 0.0), axis=1, keepdims=True)
                    out = jnp.where(lane == 16 * t + g, col, out)
            return out

        for cp in small:
            cp.wait()
        bv = jnp.zeros((1, 128), jnp.float32)
        for m in range(NM):
            q = mats[m]
            w = wbuf[m][...]
            part = jnp.sum(w * w, axis=(0, 1), keepdims=True) * (1.0 / q['size'])
            bv = jnp.where(lane1 == 2 * NM + m, part, bv)
            rows_of(vrbuf[m], q['rows_b'], 2 * m)
            rows_of(vcbuf[m], cols[m], 2 * m + 1)
            if q['flip']:
                vrc[m] = stage[2 * m]
                vcc[m] = to_compact(2 * m + 1, q['n0'])
            else:
                vrc[m] = to_compact(2 * m, q['n0'])
                vcc[m] = stage[2 * m + 1]

        for i in range(2):
            signal_z(greet.at[i])
            pl.semaphore_wait(greet.at[i], n_z)

        n_rc = [(q['lanes'], 8) if q['flip'] else (8, q['lanes']) for q in mats]

        def send_rows(m):
            n_r = n_rc[m][0]
            for k in (3, 1, 2):
                remote(rmsg.at[m, pl.ds(0, n_r)], rrx.at[3 * m + k - 1, pl.ds(0, n_r)], a_s.at[0], ra_r.at[m],
                       model=lax.rem(z + k, n_model)).start()

        def send_cols(m):
            n_c = n_rc[m][1]
            if n_c == 8:
                remote(cmsg.at[m], csib.at[m], a_s.at[0], cs_r.at[m], data=sib).start()
                return
            for k in range(n_data - 1, 0, -1):
                remote(cmsg.at[m, pl.ds(0, n_c)], crx.at[7 * m + k - 1, pl.ds(0, n_c)], a_s.at[0], ca_r.at[m],
                       data=lax.rem(d + k, n_data)).start()

        def share_pair(m):
            wait_bytes(csib.at[m], cs_r.at[m])
            csib[m] = csib[m] + cmsg[m]
            for k, peer in enumerate((dd, dx, dy)):
                remote(csib.at[m], crx.at[7 * m + k], a_s.at[0], ca_r.at[m], data=peer).start()

        a_rows = sum(3 * r + (32 if c == 8 else 7 * c) for r, c in n_rc)

        def finish_sum(m):
            q = mats[m]
            half, n1 = q['half'], q['n1']
            acc1 = jnp.zeros((8, n1), jnp.float32)
            rsums = []
            fetch_done(whole[m, OWN])
            for h in range(2):
                arrived(m, 1 + h)
                arrived(m, 4 + h)
                rows = slice(h * half, (h + 1) * half)
                total = loc[m][OWN, rows, :] + rec[m][OWN, rows, :] + fxy[m][1 + h] + fxy[m][4 + h]
                upd[m][rows, :] = total
                sq = (total * total + 1e-30).reshape(half // 8, 8, n1)
                acc1 = acc1 + jnp.sum(sq, axis=0)
                rsums.append(jnp.sum(sq, axis=2, keepdims=True))
            sum1 = jnp.sum(acc1, axis=0, keepdims=True)
            msg0, msg1 = (cmsg, rmsg) if q['flip'] else (rmsg, cmsg)
            msg0[m] = compact(jnp.concatenate(rsums, axis=0))
            for k in range(q['lanes']):
                msg1[m, k:k + 1, :] = sum1[:, 128 * k:128 * k + 128]
            send_rows(m)
            send_cols(m)

        def apply_factors(m, bv, locrow):
            q = mats[m]
            n_r, n_c = n_rc[m]
            rtot = rmsg[m, 0:n_r, :]
            wait_bytes(rrx.at[pl.ds(3 * m, 3), pl.ds(0, n_r)], ra_r.at[m])
            for k in range(3):
                rtot = rtot + rrx[3 * m + k, 0:n_r, :]
            n_in = 3 if n_c == 8 else 7
            ctot = csib[m] if n_c == 8 else cmsg[m, 0:n_c, :]
            wait_bytes(crx.at[pl.ds(7 * m, n_in), pl.ds(0, n_c)], ca_r.at[m])
            for k in range(n_in):
                ctot = ctot + crx[7 * m + k, 0:n_c, :]
            vr = BETA * vrc[m, 0:n_r, :] + (1.0 - BETA) * (rtot * (1.0 / q['cols_t']))
            vc = BETA * vcc[m, 0:n_c, :] + (1.0 - BETA) * (ctot * (1.0 / q['rows_t']))
            ok = lane < q['groups']
            if q['flip']:
                vr_sum = jnp.sum(vr, axis=(0, 1), keepdims=True)
            else:
                vr_sum = jnp.sum(jnp.where(ok, vr, 0.0), axis=(0, 1), keepdims=True)
            mloc = vr_sum * (1.0 / q['rows_b'])
            if q['flip']:
                fac0 = lax.rsqrt(jnp.where(ok, vc, 1.0))
                fac1 = lax.rsqrt(vr / mloc)
                vcc[m] = vc
                stats[1 + 2 * m, 0:n_r, :] = vr
            else:
                fac0 = lax.rsqrt(jnp.where(ok, vr / mloc, 1.0))
                fac1 = lax.rsqrt(vc)
                vcc[m] = vr
                stats[1 + 2 * m, 0:n_c, :] = vc
            f1 = jnp.concatenate([jnp.broadcast_to(fac1[k:k + 1, :], (8, 128)) for k in range(q['lanes'])], axis=1)
            g_n = q['groups']
            f0 = expand(fac0, g_n)
            u = upd[m][...].reshape(g_n, 8, q['n1']) * f0 * f1[None]
            upd[m][...] = u.reshape(q['n0'], q['n1'])
            t_m = jnp.sum(jnp.sum(u * u, axis=0), axis=(0, 1), keepdims=True) * (1.0 / q['size'])
            bv = jnp.where(lane1 == m, t_m / mloc, bv)
            bv = jnp.where(lane1 == NM + m, vr_sum * (1.0 / (q['rows_t'] * n_model)), bv)
            locrow = jnp.where(lane1 == m, mloc, locrow)
            return bv, locrow

        locrow = jnp.ones((1, 128), jnp.float32)
        send_acc(0)
        send_raw(2)
        send_acc(1)
        finish_sum(0)
        send_raw(3)
        share_pair(0)
        send_acc(2)
        finish_sum(1)
        share_pair(1)
        send_acc(3)
        bv, locrow = apply_factors(0, bv, locrow)
        finish_sum(2)
        bv, locrow = apply_factors(1, bv, locrow)
        finish_sum(3)
        bv, locrow = apply_factors(2, bv, locrow)
        bv, locrow = apply_factors(3, bv, locrow)

        brx[0:1, :] = bv
        for kz in (3, 1, 2, 0):
            for kd in range(n_data - 1, -1, -1):
                if kz == 0 and kd == 0:
                    continue
                i = kz * n_data + kd
                remote(brx.at[pl.ds(0, 1), :], brx.at[pl.ds(i, 1), :], b_s.at[0], b_r.at[0],
                       data=lax.rem(d + kd, n_data), model=lax.rem(z + kz, n_model)).start()

        for m in range(NM):
            q = mats[m]
            wide = expand(vcc[m], q['groups'])
            for t in range(q['tiles']):
                n_t = min(128, q['n0'] - 128 * t)
                g_n = n_t // 8
                shape = (g_n, 8, 128)
                pick = (lax.broadcasted_iota(jnp.int32, shape, 2)
                        == 8 * lax.broadcasted_iota(jnp.int32, shape, 0) + lax.broadcasted_iota(jnp.int32, shape, 1))
                rows = jnp.sum(jnp.where(pick, wide[16 * t:16 * t + g_n], 0.0), axis=0)
                stats[2 + 2 * m, t:t + 1, :] = jnp.sum(rows, axis=0, keepdims=True)

        for m in range(NM):
            wait_bytes(rec[m], dd_s.at[m])
            wait_bytes(fxy[m], l_s.at[m])
        wait_bytes(loc[0].at[0, pl.ds(0, a_rows), :], a_s.at[0])
        wait_bytes(brx.at[pl.ds(1, n_model * n_data - 1), :], b_r.at[0])
        tot = jnp.broadcast_to(jnp.sum(brx[...], axis=0, keepdims=True), (8, 128))
        mean_vr = pltpu.roll(tot, 128 - NM, 1)
        u_rms = jnp.sqrt(mean_vr * tot)
        w_rms = jnp.sqrt(pltpu.roll(tot, 128 - 2 * NM, 1))
        fac = -(LR_REL * jnp.maximum(1e-3, w_rms)) * (jnp.sqrt(mean_vr) * lax.rsqrt(locrow))
        stats[0] = fac / jnp.maximum(1.0, u_rms)
        wait_bytes(brx.at[pl.ds(1, n_model * n_data - 1), :], b_s.at[0])

    f32 = jnp.float32
    dma = pltpu.SemaphoreType.DMA
    vm = pltpu.VMEM
    scratch = []
    scratch += [vm((4, q['n0'], q['n1']), f32) for q in mats]
    scratch += [vm((4, q['n0'], q['n1']), f32) for q in mats]
    scratch += [vm((6, q['half'], q['n1']), f32) for q in mats]
    scratch += [vm((r,), f32) for r in rows_b]
    scratch += [vm((c,), f32) for c in cols]
    scratch += [vm((mats[0]['n0'], mats[0]['n1']), f32)]
    tile = lambda *lead: vm((*lead, 8, 128), f32)
    scratch += [tile(NM), tile(3 * NM), tile(NM), tile(7 * NM), tile(NM), vm((n_model * n_data, 128), f32),
                tile(NM), tile(NM), tile(2 * NM)]
    scratch += [dma((13,)), dma((NM,)), dma((len(fetches),)), dma((NM,)), dma((6 * NM,)), dma((3 * NM,)),
                dma((1,)), dma((NM,)), dma((NM,)), dma((2,)), dma((1,)), dma((1,)), pltpu.SemaphoreType.REGULAR((2,))]
    blocks = [jax.ShapeDtypeStruct((q['n0'], q['n1']), f32) for q in mats]
    out_shape = blocks + blocks + [jax.ShapeDtypeStruct((1 + 2 * NM, 8, 128), f32)]
    vmem = pl.BlockSpec(memory_space=pltpu.VMEM)
    hbm = pl.BlockSpec(memory_space=pltpu.HBM)
    return pl.pallas_call(
        kernel, out_shape=out_shape, in_specs=[hbm] * 16, out_specs=[vmem] * len(out_shape),
        scratch_shapes=scratch,
        compiler_params=pltpu.CompilerParams(collective_id=0, has_side_effects=True,
                                             vmem_limit_bytes=28 * 1024 * 1024))


def make_apply_kernel(rows_b, cols, n_model, n_data):
    mats = layout_of(rows_b, cols, n_model, n_data)

    def kernel(*refs):
        upd, params, stats = refs[0:4], refs[4:8], refs[8]
        new, delta, vrow_out, vcol_out = refs[9:13], refs[13:17], refs[17:21], refs[21:25]
        bufs, vrbuf, vcbuf = refs[25:33], refs[33:37], refs[37:41]
        sem = refs[41]
        copies = []

        def put(src, dst, i):
            copies.append(pltpu.make_async_copy(src, dst, sem.at[i]))
            copies[-1].start()

        for m in range(NM):
            fac = stats[0, 0:1, m:m + 1]
            step = fac * upd[m][...]
            bufs[4 + m][...] = step
            put(bufs[4 + m], delta[m], 4 + m)
            bufs[m][...] = params[m][...] + step
            put(bufs[m], new[m], m)
        for m in range(NM):
            q = mats[m]
            out1, out0 = (vrbuf[m], vcbuf[m]) if q['flip'] else (vcbuf[m], vrbuf[m])
            for k in range(q['lanes']):
                out1[pl.ds(128 * k, 128)] = stats[1 + 2 * m, k:k + 1, :].reshape(128)
            for t in range(q['tiles']):
                n_t = min(128, q['n0'] - 128 * t)
                out0[pl.ds(128 * t, n_t)] = stats[2 + 2 * m, t:t + 1, 0:n_t].reshape(n_t)
            put(vrbuf[m], vrow_out[m], 8 + m)
            put(vcbuf[m], vcol_out[m], 12 + m)
        for cp in copies:
            cp.wait()

    f32 = jnp.float32
    vmem = pl.BlockSpec(memory_space=pltpu.VMEM)
    hbm = pl.BlockSpec(memory_space=pltpu.HBM)
    blocks = [jax.ShapeDtypeStruct((q['n0'], q['n1']), f32) for q in mats]
    out_shape = (blocks + blocks + [jax.ShapeDtypeStruct((r,), f32) for r in rows_b]
                 + [jax.ShapeDtypeStruct((c,), f32) for c in cols])
    scratch = [pltpu.VMEM((q['n0'], q['n1']), f32) for q in mats] * 2
    scratch += [pltpu.VMEM((n,), f32) for n in (*rows_b, *cols)] + [pltpu.SemaphoreType.DMA((16,))]
    return pl.pallas_call(
        kernel, out_shape=out_shape, in_specs=[vmem] * 9, out_specs=[hbm] * 16, scratch_shapes=scratch,
        compiler_params=pltpu.CompilerParams(vmem_limit_bytes=6 * 1024 * 1024))


def solution(mesh):
    n_data = mesh.shape['data']
    n_model = mesh.shape['model']
    mat_spec = P('data', 'model')
    in_specs = (P('data', None, 'model'), mat_spec, P('data'), P('model')) * NM
    out_specs = (mat_spec, mat_spec, P('data'), P('model')) * NM

    def per_device(*arrays):
        grads, params = arrays[0::4], arrays[1::4]
        rows_b = [p.shape[0] for p in params]
        cols = [p.shape[1] for p in params]
        mats = layout_of(rows_b, cols, n_model, n_data)
        view = lambda i, a: jnp.swapaxes(a, -1, -2) if mats[i]['flip'] else a
        grads = [view(i, g) for i, g in enumerate(grads)]
        params = [view(i, p) for i, p in enumerate(params)]
        pin = lambda a: pltpu.with_memory_space_constraint(a, pltpu.HBM)
        outs = make_reduce_kernel(rows_b, cols, n_model, n_data)(
            *map(pin, grads), *map(pin, params), *map(pin, arrays[2::4]), *map(pin, arrays[3::4]))
        res = make_apply_kernel(rows_b, cols, n_model, n_data)(*outs)
        flat = []
        for m in range(NM):
            flat += [view(m, res[m]), view(m, res[4 + m]), res[8 + m], res[12 + m]]
        return tuple(flat)

    return jax.shard_map(per_device, mesh=mesh, in_specs=in_specs, out_specs=out_specs, check_vma=False)
```

time: 299 us -> 58.8 us (0.20)
  waiting for transfers between devices: 180 us -> 0 us
  blocking collectives: 72.2 us -> 0 us
  Pallas kernels: 0 us -> 57.9 us
  other arithmetic: 22.5 us -> 0 us
  between operations: 22.1 us -> 0.66 us
    reduce_scatter x4 -> x0, waiting for transfers between devices: 178 us -> none  [shard_update(): lax.psum_scatter(grad_rep[0], 'data', scatter_dimension=0, tiled=True)]
    psum x3 -> x0, blocking collectives: 72.2 us -> none  [the longest x1 38 us: shard_update(): lax.psum(jnp.sum(update * update), ('model', 'data')) / entries]
    pallas_call x0 -> x2, Pallas kernels: none -> 57.9 us  [the longest x1 56.3 us: per_device(): make_reduce_kernel(rows_b, cols, n_model, n_data)]
    reduce_sum x14 -> x0, other arithmetic: 15.3 us -> none  [the longest x4 6.88 us: shard_update(): jnp.sum(update * update)]
    add x4 -> x0, other arithmetic: 4.81 us -> none  [shard_update(): return (param + delta, delta, vrow_new, vcol_new)]
  transfers between devices with their start and end apart: 4 -> 0, of which waited for: 4 -> 0; matrix products, arithmetic and copies ran while one was open for 2% -> 0% of each run, Pallas kernels for 0% -> 0%
where the time goes in v3:
time: 58.8 us; the launch traced here: 58.6 us
  Pallas kernels  57.9 us (98%)
  between operations  0.66 us (1%)
    pallas_call x1, Pallas kernels, per_device(): make_reduce_kernel(rows_b, cols, n_model, n_data)  56.3 us
    pallas_call x1, Pallas kernels, per_device(): res = make_apply_kernel(rows_b, cols, n_model, n_data)(*outs)  1.64 us

profile of v3, /device:TPU:0, one launch (start us, length us, event | category | flops | bytes accessed | tf_op | source)
XLA Modules:
  0.0 58.6 jit_solution(7133950801290814083)
XLA Ops:
  0.7 56.3 %shard_map.279 = (f32[704,128]{1,0:T(8,128)S(1)}, f32[704,128]{1,0:T(8,128)S(1)}, f32[352,256]{1,0:T(8,128)S(1)}, f32[128,256]{1,0:T(8,128)S(1)}, f32[704,128]{1...) custom-call(f32[1,704,1024]{2,1,0:T(8,128)} %bitcast.8, ...), custom_call_target="tpu_custom_call" | custom-call | tf_op jit(solution)/shard_map/pallas_call | solution.py:479
  57.0 1.6 %shard_map.280 = (f32[704,128]{1,0:T(8,128)}, f32[704,128]{1,0:T(8,128)}, f32[352,256]{1,0:T(8,128)}, f32[128,256]{1,0:T(8,128)}, f32[704,128]{1,0:T(8,128)}, /*...) custom-call(f32[704,128]{1,0:T(8,128)S(1)} %get-tuple-element.41.ref, ...), custom_call_target="tpu_custom_call" | custom-call | tf_op jit(solution)/shard_map/pallas_call | solution.py:481

commit v4 on v3

--- a/solution.py
+++ b/solution.py
@@ -31,15 +31,7 @@
     first = []
     for lo, hi in ((0, FIRST_ROWS), (FIRST_ROWS, halves[0])):
         first += [(0, ND, lo, hi - lo), (0, ND, halves[0] + lo, hi - lo)]
-    whole = {(m, j): (m, j, 0, mats[m]['n0']) for m in range(NM) for j in (OWN, NX, NY, ND) if (m, j) != (0, ND)}
-    fetches = first + list(whole.values())
-    index = {f: i for i, f in enumerate(fetches)}
-    ld_slot = {f: i for i, f in enumerate(first)}
-    for m in range(NM):
-        for i, j in enumerate((ND, NX, NY)):
-            if (m, j) in whole:
-                ld_slot[whole[m, j]] = {0: 3 + i, 1: 6 + i, 2: (0, 4, 5)[i], 3: 6 + i}[m]
-        ld_slot[whole[m, OWN]] = 9 + m
+    group = {m: [(m, j, 0, mats[m]['n0']) for j in ((NX, NY, OWN) if m == 0 else (ND, NX, NY, OWN))] for m in range(NM)}
 
     def kernel(*refs):
         grads = refs[0:4]
@@ -53,7 +45,7 @@
         take = lambda n: [sc.pop(0) for _ in range(n)]
         loc, rec, fxy, vrbuf, vcbuf = (take(4) for _ in range(5))
         stg, rmsg, rrx, cmsg, crx, csib, brx, vrc, vcc, stage = take(10)
-        ld_sem, dd_s, dd_r, l_s, l_r, in_sem, a_s, ra_r, ca_r, cs_r, b_s, b_r, greet = take(13)
+        ld_sem, dd_s, dd_r, l_s, l_r, a_s, a_r, cs_r, b_s, b_r, greet = take(11)
 
         z = lax.axis_index('model')
         d = lax.axis_index('data')
@@ -109,35 +101,39 @@
             return grads[m].at[0, pl.ds(pl.multiple_of(who * q['n0'] + r0, 8), n), :]
 
         loads, dsend, stage_in = {}, {}, {}
-        for f in fetches:
+        for f in first + group[0] + group[1] + group[2] + group[3]:
             m, j, r0, n = f
-            part = (m, pl.ds(r0, n))
-            loads[f] = pltpu.make_async_copy(block(owner[j], f), loc[m].at[j, pl.ds(r0, n), :], ld_sem.at[ld_slot[f]])
+            slot = first.index(f) if f in first else 4 + m
+            loads[f] = pltpu.make_async_copy(block(owner[j], f), loc[m].at[j, pl.ds(r0, n), :], ld_sem.at[slot])
             source = block(owner[j] + sib_step, f)
             if f in first:
                 held = stg.at[pl.ds(r0, n), :]
-                stage_in[f] = pltpu.make_async_copy(source, held, ld_sem.at[9 + first.index(f)])
+                stage_in[f] = pltpu.make_async_copy(source, held, ld_sem.at[4 + slot])
                 source = held
-            dsend[f] = remote(source, rec[m].at[j, pl.ds(r0, n), :], dd_s.at[m], dd_r.at[index[f]], data=sib)
+            dsend[f] = remote(source, rec[m].at[j, pl.ds(r0, n), :], dd_s.at[m], dd_r.at[slot], data=sib)
 
         def fetch(pieces):
             for f in pieces:
                 dsend[f].start()
                 loads[f].start()
 
-        def fetch_done(f):
-            loads[f].wait()
-            dsend[f].wait_recv()
+        def fetch_done(m):
+            some = pl.ds(0, 3) if m == 0 else pl.ds(0, 4)
+            wait_bytes(loc[m].at[some], ld_sem.at[4 + m])
+            wait_bytes(rec[m].at[some], dd_r.at[4 + m])
 
         def link_send(m, j, r0, n):
             h, off = (0, r0) if r0 < halves[m] else (1, r0 - halves[m])
             along_x = (j == ND and h == 0) or j == NX
-            slot = (0 if along_x else 3) + (0 if j == ND else 1 + h)
+            slot = (0 if along_x else 1) if j == ND else (2 if along_x else 4) + h
             return remote(loc[m].at[j, pl.ds(r0, n), :], fxy[m].at[slot, pl.ds(off, n), :],
-                          l_s.at[m], l_r.at[6 * m + slot], data=dx if along_x else dy)
-
-        def arrived(m, slot):
-            wait_bytes(fxy[m].at[slot], l_r.at[6 * m + slot])
+                          l_s.at[m], l_r.at[2 * m + (0 if j == ND else 1)], data=dx if along_x else dy)
+
+        def relays_in(m):
+            wait_bytes(fxy[m].at[pl.ds(0, 2)], l_r.at[2 * m])
+
+        def finals_in(m):
+            wait_bytes(fxy[m].at[pl.ds(2, 4)], l_r.at[2 * m + 1])
 
         def pair_sum(m, j, r0, n, relay=None):
             total = loc[m][j, r0:r0 + n, :] + rec[m][j, r0:r0 + n, :]
@@ -148,24 +144,18 @@
 
         def send_raw(m):
             n = halves[m]
-            fetch_done(whole[m, ND])
-            pair_sum(m, ND, 0, n)
-            pair_sum(m, ND, n, n)
-            send_near(m)
-
-        def send_near(m):
-            n = halves[m]
-            fetch_done(whole[m, NX])
+            fetch_done(m)
+            if m > 0:
+                pair_sum(m, ND, 0, n)
+                pair_sum(m, ND, n, n)
             pair_sum(m, NX, 0, n)
-            fetch_done(whole[m, NY])
             pair_sum(m, NY, n, n)
 
         def send_acc(m):
             n = halves[m]
-            arrived(m, 0)
+            relays_in(m)
             pair_sum(m, NY, 0, n, 0)
-            arrived(m, 3)
-            pair_sum(m, NX, n, n, 3)
+            pair_sum(m, NX, n, n, 1)
 
         for f in first:
             stage_in[f].start()
@@ -175,26 +165,26 @@
         for f in first:
             stage_in[f].wait()
             dsend[f].start()
-        fetch([whole[0, NX], whole[0, NY]])
-        for f in first[0:2]:
-            fetch_done(f)
+        fetch(group[0])
+        for i, f in enumerate(first):
+            loads[f].wait()
+            dsend[f].wait_recv()
             pair_sum(*f)
-        fetch([whole[1, ND], whole[1, NX], whole[1, NY]])
-        for f in first[2:4]:
-            fetch_done(f)
-            pair_sum(*f)
-        send_near(0)
-        fetch([whole[2, ND], whole[2, NX], whole[2, NY]])
+            if i == 1:
+                fetch(group[1])
+        send_raw(0)
+        fetch(group[2])
         send_raw(1)
-        fetch([whole[3, ND], whole[3, NX], whole[3, NY]])
-        fetch([whole[m, OWN] for m in range(NM)])
-        small = []
-        for m in range(NM):
-            small.append(pltpu.make_async_copy(params[m], wbuf[m], in_sem.at[m]))
-            small.append(pltpu.make_async_copy(vrows[m], vrbuf[m], in_sem.at[4 + m]))
-            small.append(pltpu.make_async_copy(vcols[m], vcbuf[m], in_sem.at[8 + m]))
-        for cp in small:
-            cp.start()
+        fetch(group[3])
+        small = [pltpu.make_async_copy(vrows[m], vrbuf[m], ld_sem.at[m]) for m in range(NM)]
+        small += [pltpu.make_async_copy(vcols[m], vcbuf[m], ld_sem.at[4 + m]) for m in range(2)]
+        late = [pltpu.make_async_copy(params[m], wbuf[m], ld_sem.at[m]) for m in range(NM)]
+        late += [pltpu.make_async_copy(vcols[m], vcbuf[m], ld_sem.at[2 + m]) for m in range(2, NM)]
+        for turn in (small, late):
+            for cp in turn:
+                cp.start()
+            for cp in turn:
+                cp.wait()
 
         lane = lax.broadcasted_iota(jnp.int32, (8, 128), 1)
         sub = lax.broadcasted_iota(jnp.int32, (8, 128), 0)
@@ -225,8 +215,6 @@
                     out = jnp.where(lane == 16 * t + g, col, out)
             return out
 
-        for cp in small:
-            cp.wait()
         bv = jnp.zeros((1, 128), jnp.float32)
         for m in range(NM):
             q = mats[m]
@@ -251,7 +239,7 @@
         def send_rows(m):
             n_r = n_rc[m][0]
             for k in (3, 1, 2):
-                remote(rmsg.at[m, pl.ds(0, n_r)], rrx.at[3 * m + k - 1, pl.ds(0, n_r)], a_s.at[0], ra_r.at[m],
+                remote(rmsg.at[m, pl.ds(0, n_r)], rrx.at[3 * m + k - 1, pl.ds(0, n_r)], a_s.at[0], a_r.at[m],
                        model=lax.rem(z + k, n_model)).start()
 
         def send_cols(m):
@@ -260,14 +248,14 @@
                 remote(cmsg.at[m], csib.at[m], a_s.at[0], cs_r.at[m], data=sib).start()
                 return
             for k in range(n_data - 1, 0, -1):
-                remote(cmsg.at[m, pl.ds(0, n_c)], crx.at[7 * m + k - 1, pl.ds(0, n_c)], a_s.at[0], ca_r.at[m],
+                remote(cmsg.at[m, pl.ds(0, n_c)], crx.at[7 * m + k - 1, pl.ds(0, n_c)], a_s.at[0], a_r.at[m],
                        data=lax.rem(d + k, n_data)).start()
 
         def share_pair(m):
             wait_bytes(csib.at[m], cs_r.at[m])
             csib[m] = csib[m] + cmsg[m]
             for k, peer in enumerate((dd, dx, dy)):
-                remote(csib.at[m], crx.at[7 * m + k], a_s.at[0], ca_r.at[m], data=peer).start()
+                remote(csib.at[m], crx.at[7 * m + k], a_s.at[0], a_r.at[m], data=peer).start()
 
         a_rows = sum(3 * r + (32 if c == 8 else 7 * c) for r, c in n_rc)
 
@@ -276,12 +264,10 @@
             half, n1 = q['half'], q['n1']
             acc1 = jnp.zeros((8, n1), jnp.float32)
             rsums = []
-            fetch_done(whole[m, OWN])
+            finals_in(m)
             for h in range(2):
-                arrived(m, 1 + h)
-                arrived(m, 4 + h)
                 rows = slice(h * half, (h + 1) * half)
-                total = loc[m][OWN, rows, :] + rec[m][OWN, rows, :] + fxy[m][1 + h] + fxy[m][4 + h]
+                total = loc[m][OWN, rows, :] + rec[m][OWN, rows, :] + fxy[m][2 + h] + fxy[m][4 + h]
                 upd[m][rows, :] = total
                 sq = (total * total + 1e-30).reshape(half // 8, 8, n1)
                 acc1 = acc1 + jnp.sum(sq, axis=0)
@@ -298,12 +284,11 @@
             q = mats[m]
             n_r, n_c = n_rc[m]
             rtot = rmsg[m, 0:n_r, :]
-            wait_bytes(rrx.at[pl.ds(3 * m, 3), pl.ds(0, n_r)], ra_r.at[m])
+            n_in = 3 if n_c == 8 else 7
+            wait_bytes(loc[0].at[0, pl.ds(0, 3 * n_r + n_in * n_c), :], a_r.at[m])
             for k in range(3):
                 rtot = rtot + rrx[3 * m + k, 0:n_r, :]
-            n_in = 3 if n_c == 8 else 7
             ctot = csib[m] if n_c == 8 else cmsg[m, 0:n_c, :]
-            wait_bytes(crx.at[pl.ds(7 * m, n_in), pl.ds(0, n_c)], ca_r.at[m])
             for k in range(n_in):
                 ctot = ctot + crx[7 * m + k, 0:n_c, :]
             vr = BETA * vrc[m, 0:n_r, :] + (1.0 - BETA) * (rtot * (1.0 / q['cols_t']))
@@ -400,8 +385,8 @@
     tile = lambda *lead: vm((*lead, 8, 128), f32)
     scratch += [tile(NM), tile(3 * NM), tile(NM), tile(7 * NM), tile(NM), vm((n_model * n_data, 128), f32),
                 tile(NM), tile(NM), tile(2 * NM)]
-    scratch += [dma((13,)), dma((NM,)), dma((len(fetches),)), dma((NM,)), dma((6 * NM,)), dma((3 * NM,)),
-                dma((1,)), dma((NM,)), dma((NM,)), dma((2,)), dma((1,)), dma((1,)), pltpu.SemaphoreType.REGULAR((2,))]
+    scratch += [dma((8,)), dma((NM,)), dma((8,)), dma((NM,)), dma((2 * NM,)), dma((1,)), dma((NM,)), dma((2,)),
+                dma((1,)), dma((1,)), pltpu.SemaphoreType.REGULAR((2,))]
     blocks = [jax.ShapeDtypeStruct((q['n0'], q['n1']), f32) for q in mats]
     out_shape = blocks + blocks + [jax.ShapeDtypeStruct((1 + 2 * NM, 8, 128), f32)]
     vmem = pl.BlockSpec(memory_space=pltpu.VMEM)
@@ -419,21 +404,16 @@
     def kernel(*refs):
         upd, params, stats = refs[0:4], refs[4:8], refs[8]
         new, delta, vrow_out, vcol_out = refs[9:13], refs[13:17], refs[17:21], refs[21:25]
-        bufs, vrbuf, vcbuf = refs[25:33], refs[33:37], refs[37:41]
-        sem = refs[41]
-        copies = []
-
-        def put(src, dst, i):
-            copies.append(pltpu.make_async_copy(src, dst, sem.at[i]))
-            copies[-1].start()
-
+        bufs, vrbuf, vcbuf = refs[25:29], refs[29:33], refs[33:37]
+        sem = refs[37]
         for m in range(NM):
             fac = stats[0, 0:1, m:m + 1]
             step = fac * upd[m][...]
-            bufs[4 + m][...] = step
-            put(bufs[4 + m], delta[m], 4 + m)
-            bufs[m][...] = params[m][...] + step
-            put(bufs[m], new[m], m)
+            bufs[m][0] = step
+            pltpu.make_async_copy(bufs[m].at[0], delta[m], sem.at[m]).start()
+            bufs[m][1] = params[m][...] + step
+            pltpu.make_async_copy(bufs[m].at[1], new[m], sem.at[m]).start()
+        copies = []
         for m in range(NM):
             q = mats[m]
             out1, out0 = (vrbuf[m], vcbuf[m]) if q['flip'] else (vcbuf[m], vrbuf[m])
@@ -442,8 +422,11 @@
             for t in range(q['tiles']):
                 n_t = min(128, q['n0'] - 128 * t)
                 out0[pl.ds(128 * t, n_t)] = stats[2 + 2 * m, t:t + 1, 0:n_t].reshape(n_t)
-            put(vrbuf[m], vrow_out[m], 8 + m)
-            put(vcbuf[m], vcol_out[m], 12 + m)
+            for i, (buf, out) in enumerate(((vrbuf[m], vrow_out[m]), (vcbuf[m], vcol_out[m]))):
+                copies.append(pltpu.make_async_copy(buf, out, sem.at[NM + 2 * m + i]))
+                copies[-1].start()
+        for m in range(NM):
+            pltpu.make_async_copy(bufs[m], bufs[m], sem.at[m]).wait()
         for cp in copies:
             cp.wait()
 
@@ -453,8 +436,8 @@
     blocks = [jax.ShapeDtypeStruct((q['n0'], q['n1']), f32) for q in mats]
     out_shape = (blocks + blocks + [jax.ShapeDtypeStruct((r,), f32) for r in rows_b]
                  + [jax.ShapeDtypeStruct((c,), f32) for c in cols])
-    scratch = [pltpu.VMEM((q['n0'], q['n1']), f32) for q in mats] * 2
-    scratch += [pltpu.VMEM((n,), f32) for n in (*rows_b, *cols)] + [pltpu.SemaphoreType.DMA((16,))]
+    scratch = [pltpu.VMEM((2, q['n0'], q['n1']), f32) for q in mats]
+    scratch += [pltpu.VMEM((n,), f32) for n in (*rows_b, *cols)] + [pltpu.SemaphoreType.DMA((3 * NM,))]
     return pl.pallas_call(
         kernel, out_shape=out_shape, in_specs=[vmem] * 9, out_specs=[hbm] * 16, scratch_shapes=scratch,
         compiler_params=pltpu.CompilerParams(vmem_limit_bytes=6 * 1024 * 1024))

time: 58.8 us -> 58.2 us (0.990)
  no operation moved by 1% of the time
where the time goes in v4:
time: 58.2 us; the launch traced here: 58.1 us
  Pallas kernels  57.4 us (99%)
  between operations  0.66 us (1%)
    pallas_call x1, Pallas kernels, per_device(): make_reduce_kernel(rows_b, cols, n_model, n_data)  55.8 us
    pallas_call x1, Pallas kernels, per_device(): res = make_apply_kernel(rows_b, cols, n_model, n_data)(*outs)  1.61 us

profile of v4, /device:TPU:0, one launch (start us, length us, event | category | flops | bytes accessed | tf_op | source)
XLA Modules:
  0.0 58.1 jit_solution(1054077588458857314)
XLA Ops:
  0.7 55.8 %shard_map.279 = (f32[704,128]{1,0:T(8,128)S(1)}, f32[704,128]{1,0:T(8,128)S(1)}, f32[352,256]{1,0:T(8,128)S(1)}, f32[128,256]{1,0:T(8,128)S(1)}, f32[704,128]{1...) custom-call(f32[1,704,1024]{2,1,0:T(8,128)} %bitcast.8, ...), custom_call_target="tpu_custom_call" | custom-call | tf_op jit(solution)/shard_map/pallas_call | solution.py:462
  56.4 1.6 %shard_map.280 = (f32[704,128]{1,0:T(8,128)}, f32[704,128]{1,0:T(8,128)}, f32[352,256]{1,0:T(8,128)}, f32[128,256]{1,0:T(8,128)}, f32[704,128]{1,0:T(8,128)}, /*...) custom-call(f32[704,128]{1,0:T(8,128)S(1)} %get-tuple-element.41.ref, ...), custom_call_target="tpu_custom_call" | custom-call | tf_op jit(solution)/shard_map/pallas_call | solution.py:464

commit v5 on v4

v5 whole, which is shorter than its diff:
```python
import jax
import jax.numpy as jnp
from jax import lax
from jax.experimental import pallas as pl
from jax.experimental.pallas import tpu as pltpu
from jax.sharding import PartitionSpec as P

OPT_STEP = 3
BETA = 1.0 - OPT_STEP ** -0.8
LR_REL = min(0.01, OPT_STEP ** -0.5)
NM = 4
OWN, NX, NY, ND = 0, 1, 2, 3
FIRST_ROWS = 88
PARTS = 4
LANES = 128
TILE = (8, LANES)
MIB = 1024 * 1024
MESH_ID = pl.DeviceIdType.MESH


def layout_of(rows_b, cols, n_model, n_data):
    mats = []
    for r, c in zip(rows_b, cols):
        flip = c % LANES != 0
        n0, n1 = (c, r) if flip else (r, c)
        mats.append(dict(flip=flip, n0=n0, n1=n1, half=n0 // 2, groups=n0 // 8, tiles=-(-n0 // LANES), lanes=n1 // LANES,
                         rows_b=r, rows_t=r * n_data, cols_t=c * n_model,
                         size=float(r * n_data * c * n_model)))
    return mats


def make_reduce_kernel(rows_b, cols, n_model, n_data):
    mats = layout_of(rows_b, cols, n_model, n_data)
    halves = [q['half'] for q in mats]
    n_rc = [(q['lanes'], 8) if q['flip'] else (8, q['lanes']) for q in mats]
    sent_rows = sum(7 * q['n0'] * q['lanes'] for q in mats) + n_model * n_data - 1
    sent_rows += sum(3 * r + (24 if c == 8 else 7 * c) for r, c in n_rc)
    first = []
    for lo, hi in ((0, FIRST_ROWS), (FIRST_ROWS, halves[0])):
        first += [(0, ND, lo, hi - lo), (0, ND, halves[0] + lo, hi - lo)]
    group = {m: [(m, j, 0, mats[m]['n0']) for j in ((NX, NY, OWN) if m == 0 else (ND, NX, NY, OWN))] for m in range(NM)}

    def kernel(*refs):
        grads = refs[0:4]
        params = refs[4:8]
        vrows = refs[8:12]
        vcols = refs[12:16]
        upd = refs[16:20]
        wbuf = refs[20:24]
        stats = refs[24]
        sc = list(refs[25:])
        take = lambda n: [sc.pop(0) for _ in range(n)]
        loc, rec, fxy, vrbuf, vcbuf = (take(4) for _ in range(5))
        stg, rmsg, rrx, cmsg, crx, csib, chalf, brx, vrc, vcc, stage, sent = take(12)
        ld_sem, dd_r, l_r, ra_r, ca_r, cs_r, cm_r, b_r, s_sem, greet = take(10)

        z = lax.axis_index('model')
        d = lax.axis_index('data')
        core = lax.rem(d, 2)
        xx = lax.rem(d // 2, 2)
        yy = d // 4
        sib_step = 1 - 2 * core
        sib = d + sib_step
        dx = d + 2 - 4 * xx
        dy = d + 4 - 8 * yy
        dd = dx + 4 - 8 * yy
        owner = {OWN: d, NX: dx, NY: dy, ND: dd}

        def flip_d(k):
            return d + (k % 2) * sib_step + (k // 2 % 2) * (2 - 4 * xx) + (k // 4) * (4 - 8 * yy)

        def flip_z(k):
            return z + (k % 2) * (1 - 2 * lax.rem(z, 2)) + (k // 2) * (2 - 4 * (z // 2))

        def remote(src, dst, ssem, rsem, data=None, model=None):
            return pltpu.make_async_remote_copy(
                src_ref=src, dst_ref=dst, send_sem=ssem, recv_sem=rsem,
                device_id=(z if model is None else model, d if data is None else data),
                device_id_type=MESH_ID)

        def signal(sem, data=None, model=None):
            pl.semaphore_signal(
                sem, inc=1,
                device_id=(z if model is None else model, d if data is None else data),
                device_id_type=MESH_ID)

        def wait_bytes(ref, sem):
            pltpu.make_async_copy(ref, ref, sem).wait()

        barrier = pltpu.get_barrier_semaphore()
        first_core, second_core = core == 0, core == 1
        up_ok = z < n_model - 1
        down_ok = z > 0
        n_z = jnp.where(up_ok, 1, 0) + jnp.where(down_ok, 1, 0)

        def signal_z(sem, data=None, also=None):
            @pl.when(up_ok if also is None else up_ok & also)
            def _():
                signal(sem, data=data, model=z + 1)

            @pl.when(down_ok if also is None else down_ok & also)
            def _():
                signal(sem, data=data, model=z - 1)

        @pl.when(second_core)
        def _():
            signal(barrier, data=sib)

        def block(who, f):
            m, j, r0, n = f
            q = mats[m]
            if q['flip']:
                cut = pl.ds(pl.multiple_of(who * q['n1'], LANES), q['n1'])
                return grads[m].at[0, pl.ds(r0, n), cut]
            return grads[m].at[0, pl.ds(pl.multiple_of(who * q['n0'] + r0, 8), n), :]

        loads, dsend, stage_in = {}, {}, {}
        for f in first + group[0] + group[1] + group[2] + group[3]:
            m, j, r0, n = f
            slot = first.index(f) if f in first else 4 + m
            loads[f] = pltpu.make_async_copy(block(owner[j], f), loc[m].at[j, pl.ds(r0, n), :], ld_sem.at[slot])
            source = block(owner[j] + sib_step, f)
            if f in first:
                held = stg.at[pl.ds(r0, n), :]
                stage_in[f] = pltpu.make_async_copy(source, held, ld_sem.at[4 + slot])
                source = held
            dsend[f] = remote(source, rec[m].at[j, pl.ds(r0, n), :], s_sem.at[0], dd_r.at[slot], data=sib)

        def fetch(pieces):
            for f in pieces:
                dsend[f].start()
                loads[f].start()

        def fetch_done(m):
            some = pl.ds(0, 3) if m == 0 else pl.ds(0, 4)
            wait_bytes(loc[m].at[some], ld_sem.at[4 + m])
            wait_bytes(rec[m].at[some], dd_r.at[4 + m])

        def link_send(m, j, r0, n):
            h, off = (0, r0) if r0 < halves[m] else (1, r0 - halves[m])
            along_x = (j == ND and h == 0) or j == NX
            slot = (0 if along_x else 1) if j == ND else (2 if along_x else 4) + h
            return remote(loc[m].at[j, pl.ds(r0, n), :], fxy[m].at[slot, pl.ds(off, n), :],
                          s_sem.at[0], l_r.at[2 * m + (0 if j == ND else 1)], data=dx if along_x else dy)

        def relays_in(m):
            wait_bytes(fxy[m].at[pl.ds(0, 2)], l_r.at[2 * m])

        def finals_in(m):
            wait_bytes(fxy[m].at[pl.ds(2, 4)], l_r.at[2 * m + 1])

        def pair_sum(m, j, r0, n, relay=None):
            total = loc[m][j, r0:r0 + n, :] + rec[m][j, r0:r0 + n, :]
            if relay is not None:
                total = total + fxy[m][relay]
            loc[m][j, r0:r0 + n, :] = total
            link_send(m, j, r0, n).start()

        def send_raw(m):
            n = halves[m]
            fetch_done(m)
            if m > 0:
                pair_sum(m, ND, 0, n)
                pair_sum(m, ND, n, n)
            pair_sum(m, NX, 0, n)
            pair_sum(m, NY, n, n)

        def send_acc(m):
            n = halves[m]
            relays_in(m)
            pair_sum(m, NY, 0, n, 0)
            pair_sum(m, NX, n, n, 1)

        for f in first:
            stage_in[f].start()
            loads[f].start()

        @pl.when(first_core)
        def _():
            pl.semaphore_wait(barrier, 1)
            signal(barrier, data=dx + 1)
            signal(barrier, data=dy + 1)
            signal(greet.at[2], data=sib)

        signal_z(barrier, data=sib, also=first_core)

        @pl.when(second_core)
        def _():
            pl.semaphore_wait(greet.at[2], 1)

        for f in first:
            stage_in[f].wait()
            dsend[f].start()

        @pl.when(second_core)
        def _():
            pl.semaphore_wait(barrier, 2 + n_z)
            signal(greet.at[3], data=sib)

        @pl.when(first_core)
        def _():
            pl.semaphore_wait(greet.at[3], 1)

        for i, f in enumerate(first):
            loads[f].wait()
            dsend[f].wait_recv()
            pair_sum(*f)
            if i == 1:
                fetch(group[0])
        fetch(group[1])
        send_raw(0)
        fetch(group[2])
        send_raw(1)
        fetch(group[3])
        small = [pltpu.make_async_copy(vrows[m], vrbuf[m], ld_sem.at[m]) for m in range(NM)]
        small += [pltpu.make_async_copy(vcols[m], vcbuf[m], ld_sem.at[4 + m]) for m in range(2)]
        late = [pltpu.make_async_copy(params[m], wbuf[m], ld_sem.at[m]) for m in range(NM)]
        late += [pltpu.make_async_copy(vcols[m], vcbuf[m], ld_sem.at[2 + m]) for m in range(2, NM)]
        for turn in (small, late):
            for cp in turn:
                cp.start()
            for cp in turn:
                cp.wait()

        lane = lax.broadcasted_iota(jnp.int32, TILE, 1)
        sub = lax.broadcasted_iota(jnp.int32, TILE, 0)
        lane1 = lax.broadcasted_iota(jnp.int32, (1, LANES), 1)

        def group_mask(g):
            shape = (g, 8, LANES)
            return lax.broadcasted_iota(jnp.int32, shape, 2) == lax.broadcasted_iota(jnp.int32, shape, 0)

        def compact(values):
            return jnp.sum(jnp.where(group_mask(values.shape[0]), values, 0.0), axis=0)

        def expand(vec, g):
            return jnp.sum(jnp.where(group_mask(g), vec[None], 0.0), axis=2, keepdims=True)

        def rows_of(buf, n, i):
            stage[i] = jnp.zeros(TILE, jnp.float32)
            for t in range(-(-n // LANES)):
                n_t = min(LANES, n - LANES * t)
                stage[i, t:t + 1, 0:n_t] = buf[pl.ds(LANES * t, n_t)].reshape(1, n_t)

        def to_compact(i, n):
            out = jnp.zeros(TILE, jnp.float32)
            for t in range(-(-n // LANES)):
                row = jnp.broadcast_to(stage[i, t:t + 1, :], TILE)
                for g in range(min(LANES, n - LANES * t) // 8):
                    col = jnp.sum(jnp.where(lane == 8 * g + sub, row, 0.0), axis=1, keepdims=True)
                    out = jnp.where(lane == 16 * t + g, col, out)
            return out

        bv = jnp.zeros((1, LANES), jnp.float32)
        for m in range(NM):
            q = mats[m]
            w = wbuf[m][...]
            part = jnp.sum(w * w, axis=(0, 1), keepdims=True) * (1.0 / q['size'])
            bv = jnp.where(lane1 == 2 * NM + m, part, bv)
            rows_of(vrbuf[m], q['rows_b'], 2 * m)
            rows_of(vcbuf[m], cols[m], 2 * m + 1)
            if q['flip']:
                vrc[m] = stage[2 * m]
                vcc[m] = to_compact(2 * m + 1, q['n0'])
            else:
                vrc[m] = to_compact(2 * m, q['n0'])
                vcc[m] = stage[2 * m + 1]

        for i in range(2):
            signal_z(greet.at[i])
            pl.semaphore_wait(greet.at[i], n_z)

        def send_rows(m):
            n_r = n_rc[m][0]
            for k in (3, 2, 1):
                remote(rmsg.at[m, pl.ds(0, n_r)], rrx.at[3 * m + k - 1, pl.ds(0, n_r)], s_sem.at[0], ra_r.at[m],
                       model=flip_z(k)).start()

        def send_cols(m, ks):
            n_c = n_rc[m][1]
            for k in ks:
                remote(cmsg.at[m, pl.ds(0, n_c)], crx.at[7 * m + k - 1, pl.ds(0, n_c)], s_sem.at[0], ca_r.at[m],
                       data=flip_d(k)).start()

        def share_pair(m):
            wait_bytes(csib.at[m], cs_r.at[m])
            mine = jnp.where(core == 0, csib[m, 0:4, :] + cmsg[m, 0:4, :], csib[m, 4:8, :] + cmsg[m, 4:8, :])
            chalf[m, 0] = mine
            for k, peer in enumerate((dd, dx, dy)):
                remote(chalf.at[m, 0], chalf.at[m, 1 + k], s_sem.at[0], ca_r.at[m], data=peer).start()

        def merge_pair(m):
            wait_bytes(chalf.at[m, pl.ds(1, 3)], ca_r.at[m])
            chalf[m, 4] = chalf[m, 0] + chalf[m, 1] + chalf[m, 2] + chalf[m, 3]
            remote(chalf.at[m, 4], chalf.at[m, 5], s_sem.at[0], cm_r.at[m], data=sib).start()

        def merged(m):
            wait_bytes(chalf.at[m, 5], cm_r.at[m])
            mine, other = chalf[m, 4], chalf[m, 5]
            return jnp.concatenate([jnp.where(core == 0, mine, other), jnp.where(core == 0, other, mine)], axis=0)


        def finish_sum(m):
            q = mats[m]
            half, n1 = q['half'], q['n1']
            acc1 = jnp.zeros((8, n1), jnp.float32)
            rsums = []
            finals_in(m)
            for h in range(2):
                rows = slice(h * half, (h + 1) * half)
                total = loc[m][OWN, rows, :] + rec[m][OWN, rows, :] + fxy[m][2 + h] + fxy[m][4 + h]
                upd[m][rows, :] = total
                sq = (total * total + 1e-30).reshape(half // 8, 8, n1)
                acc1 = acc1 + jnp.sum(sq, axis=0)
                rsums.append(jnp.sum(sq, axis=2, keepdims=True))
            sum1 = jnp.sum(acc1, axis=0, keepdims=True)
            msg0, msg1 = (cmsg, rmsg) if q['flip'] else (rmsg, cmsg)
            for k in range(q['lanes']):
                msg1[m, k:k + 1, :] = sum1[:, LANES * k:LANES * k + LANES]
            if not q['flip']:
                send_cols(m, (6, 7, 2, 4, 3, 5, 1))
            msg0[m] = compact(jnp.concatenate(rsums, axis=0))
            send_rows(m)
            if q['flip']:
                remote(cmsg.at[m], csib.at[m], s_sem.at[0], cs_r.at[m], data=sib).start()

        def apply_factors(m, bv, locrow):
            q = mats[m]
            n_r, n_c = n_rc[m]
            g_n, n1 = q['groups'], q['n1']
            ok = lane < g_n

            def along0(fac):
                return expand(fac, g_n)

            def along1(fac):
                wide = [jnp.broadcast_to(fac[k:k + 1, :], TILE) for k in range(q['lanes'])]
                return jnp.concatenate(wide, axis=1)[None]

            rtot = rmsg[m, 0:n_r, :]
            wait_bytes(loc[0].at[0, pl.ds(0, 3 * n_r), :], ra_r.at[m])
            for k in range(3):
                rtot = rtot + rrx[3 * m + k, 0:n_r, :]
            vr = BETA * vrc[m, 0:n_r, :] + (1.0 - BETA) * (rtot * (1.0 / q['cols_t']))
            vr_sum = jnp.sum(vr if q['flip'] else jnp.where(ok, vr, 0.0), axis=(0, 1), keepdims=True)
            mloc = vr_sum * (1.0 / q['rows_b'])
            inv_mloc = 1.0 / mloc
            rfac = lax.rsqrt(vr / mloc) if q['flip'] else lax.rsqrt(jnp.where(ok, vr / mloc, 1.0))
            part = upd[m][...].reshape(g_n, 8, n1) * (along1 if q['flip'] else along0)(rfac)
            if n_c == 8:
                ctot = merged(m)
            else:
                ctot = cmsg[m, 0:n_c, :]
                wait_bytes(loc[0].at[0, pl.ds(0, 7 * n_c), :], ca_r.at[m])
                for k in range(7):
                    ctot = ctot + crx[7 * m + k, 0:n_c, :]
            vc = BETA * vcc[m, 0:n_c, :] + (1.0 - BETA) * (ctot * (1.0 / q['rows_t']))
            cfac = lax.rsqrt(jnp.where(ok, vc, 1.0)) if q['flip'] else lax.rsqrt(vc)
            u = part * (along0 if q['flip'] else along1)(cfac)
            t_m = jnp.sum(jnp.sum(u * u, axis=0), axis=(0, 1), keepdims=True)
            upd[m][...] = u.reshape(q['n0'], n1)
            vcc[m] = vc if q['flip'] else vr
            stats[1 + 2 * m, 0:q['lanes'], :] = vr if q['flip'] else vc
            bv = jnp.where(lane1 == NM + m, vr_sum * (1.0 / (q['rows_t'] * n_model)), bv)
            bv = jnp.where(lane1 == m, (t_m * (1.0 / q['size'])) * inv_mloc, bv)
            locrow = jnp.where(lane1 == m, mloc, locrow)
            return bv, locrow

        locrow = jnp.ones((1, LANES), jnp.float32)
        send_acc(0)
        send_raw(2)
        send_acc(1)
        finish_sum(0)
        send_raw(3)
        share_pair(0)
        send_acc(2)
        finish_sum(1)
        share_pair(1)
        send_acc(3)
        merge_pair(0)
        bv, locrow = apply_factors(0, bv, locrow)
        finish_sum(2)
        merge_pair(1)
        finish_sum(3)
        bv, locrow = apply_factors(1, bv, locrow)
        bv, locrow = apply_factors(2, bv, locrow)
        bv, locrow = apply_factors(3, bv, locrow)

        brx[0:1, :] = bv
        for kz in (3, 2, 1, 0):
            for kd in range(n_data - 1, -1, -1):
                if kz == 0 and kd == 0:
                    continue
                i = kz * n_data + kd
                remote(brx.at[pl.ds(0, 1), :], brx.at[pl.ds(i, 1), :], s_sem.at[0], b_r.at[0],
                       data=flip_d(kd), model=flip_z(kz)).start()

        for m in range(NM):
            q = mats[m]
            wide = expand(vcc[m], q['groups'])
            for t in range(q['tiles']):
                n_t = min(LANES, q['n0'] - LANES * t)
                g_n = n_t // 8
                shape = (g_n, 8, LANES)
                pick = (lax.broadcasted_iota(jnp.int32, shape, 2)
                        == 8 * lax.broadcasted_iota(jnp.int32, shape, 0) + lax.broadcasted_iota(jnp.int32, shape, 1))
                rows = jnp.sum(jnp.where(pick, wide[16 * t:16 * t + g_n], 0.0), axis=0)
                stats[2 + 2 * m, t:t + 1, :] = jnp.sum(rows, axis=0, keepdims=True)

        wait_bytes(brx.at[pl.ds(1, n_model * n_data - 1), :], b_r.at[0])
        tot = jnp.broadcast_to(jnp.sum(brx[...], axis=0, keepdims=True), TILE)
        mean_vr = pltpu.roll(tot, LANES - NM, 1)
        u_rms = jnp.sqrt(mean_vr * tot)
        w_rms = jnp.sqrt(pltpu.roll(tot, LANES - 2 * NM, 1))
        fac = -(LR_REL * jnp.maximum(1e-3, w_rms)) * (jnp.sqrt(mean_vr) * lax.rsqrt(locrow))
        stats[0] = fac / jnp.maximum(1.0, u_rms)
        wait_bytes(sent, s_sem.at[0])

    f32 = jnp.float32
    dma = pltpu.SemaphoreType.DMA
    vm = pltpu.VMEM
    scratch = []
    scratch += [vm((4, q['n0'], q['n1']), f32) for q in mats]
    scratch += [vm((4, q['n0'], q['n1']), f32) for q in mats]
    scratch += [vm((6, q['half'], q['n1']), f32) for q in mats]
    scratch += [vm((r,), f32) for r in rows_b]
    scratch += [vm((c,), f32) for c in cols]
    scratch += [vm((mats[0]['n0'], mats[0]['n1']), f32)]
    tile = lambda *lead: vm((*lead, 8, LANES), f32)
    scratch += [tile(NM), tile(3 * NM), tile(NM), tile(7 * NM), tile(2), vm((2, 6, 4, LANES), f32), vm((n_model * n_data, LANES), f32),
                tile(NM), tile(NM), tile(2 * NM), vm((sent_rows, LANES), f32)]
    scratch += [dma((8,)), dma((8,)), dma((2 * NM,)), dma((NM,)), dma((NM,)), dma((2,)), dma((2,)), dma((1,)), dma((1,)),
                pltpu.SemaphoreType.REGULAR((4,))]
    blocks = [jax.ShapeDtypeStruct((q['n0'], q['n1']), f32) for q in mats]
    out_shape = blocks + blocks + [jax.ShapeDtypeStruct((1 + 2 * NM, 8, LANES), f32)]
    vmem = pl.BlockSpec(memory_space=pltpu.VMEM)
    hbm = pl.BlockSpec(memory_space=pltpu.HBM)
    return pl.pallas_call(
        kernel, out_shape=out_shape, in_specs=[hbm] * 16, out_specs=[vmem] * len(out_shape),
        scratch_shapes=scratch,
        compiler_params=pltpu.CompilerParams(collective_id=0, has_side_effects=True,
                                             vmem_limit_bytes=36 * MIB))


def make_apply_kernel(rows_b, cols, n_model, n_data):
    mats = layout_of(rows_b, cols, n_model, n_data)

    def kernel(*refs):
        upd, params, stats = refs[0:4], refs[4:8], refs[8]
        new, delta, vrow_out, vcol_out = refs[9:13], refs[13:17], refs[17:21], refs[21:25]
        bufs, vrbuf, vcbuf = refs[25:29], refs[29:33], refs[33:37]
        sem = refs[37]
        for m in range(NM):
            fac = stats[0, 0:1, m:m + 1]
            n = mats[m]['n0'] // PARTS
            for i in range(PARTS):
                rows = slice(i * n, i * n + n)
                step = fac * upd[m][rows, :]
                bufs[m][0, rows, :] = step
                pltpu.make_async_copy(bufs[m].at[0, rows], delta[m].at[rows], sem.at[m]).start()
                bufs[m][1, rows, :] = params[m][rows, :] + step
                pltpu.make_async_copy(bufs[m].at[1, rows], new[m].at[rows], sem.at[m]).start()
        copies = []
        for m in range(NM):
            q = mats[m]
            out1, out0 = (vrbuf[m], vcbuf[m]) if q['flip'] else (vcbuf[m], vrbuf[m])
            for k in range(q['lanes']):
                out1[pl.ds(LANES * k, LANES)] = stats[1 + 2 * m, k:k + 1, :].reshape(LANES)
            for t in range(q['tiles']):
                n_t = min(LANES, q['n0'] - LANES * t)
                out0[pl.ds(LANES * t, n_t)] = stats[2 + 2 * m, t:t + 1, 0:n_t].reshape(n_t)
            for i, (buf, out) in enumerate(((vrbuf[m], vrow_out[m]), (vcbuf[m], vcol_out[m]))):
                copies.append(pltpu.make_async_copy(buf, out, sem.at[NM + 2 * m + i]))
                copies[-1].start()
        for m in range(NM):
            pltpu.make_async_copy(bufs[m], bufs[m], sem.at[m]).wait()
        for cp in copies:
            cp.wait()

    f32 = jnp.float32
    vmem = pl.BlockSpec(memory_space=pltpu.VMEM)
    hbm = pl.BlockSpec(memory_space=pltpu.HBM)
    blocks = [jax.ShapeDtypeStruct((q['n0'], q['n1']), f32) for q in mats]
    out_shape = (blocks + blocks + [jax.ShapeDtypeStruct((r,), f32) for r in rows_b]
                 + [jax.ShapeDtypeStruct((c,), f32) for c in cols])
    scratch = [pltpu.VMEM((2, q['n0'], q['n1']), f32) for q in mats]
    scratch += [pltpu.VMEM((n,), f32) for n in (*rows_b, *cols)] + [pltpu.SemaphoreType.DMA((3 * NM,))]
    return pl.pallas_call(
        kernel, out_shape=out_shape, in_specs=[vmem] * 9, out_specs=[hbm] * 16, scratch_shapes=scratch,
        compiler_params=pltpu.CompilerParams(vmem_limit_bytes=6 * MIB))


def solution(mesh):
    n_data = mesh.shape['data']
    n_model = mesh.shape['model']
    mat_spec = P('data', 'model')
    in_specs = (P('data', None, 'model'), mat_spec, P('data'), P('model')) * NM
    out_specs = (mat_spec, mat_spec, P('data'), P('model')) * NM

    def per_device(*arrays):
        grads, params = arrays[0::4], arrays[1::4]
        rows_b = [p.shape[0] for p in params]
        cols = [p.shape[1] for p in params]
        mats = layout_of(rows_b, cols, n_model, n_data)
        view = lambda i, a: jnp.swapaxes(a, -1, -2) if mats[i]['flip'] else a
        grads = [view(i, g) for i, g in enumerate(grads)]
        params = [view(i, p) for i, p in enumerate(params)]
        pin = lambda a: pltpu.with_memory_space_constraint(a, pltpu.HBM)
        outs = make_reduce_kernel(rows_b, cols, n_model, n_data)(
            *map(pin, grads), *map(pin, params), *map(pin, arrays[2::4]), *map(pin, arrays[3::4]))
        res = make_apply_kernel(rows_b, cols, n_model, n_data)(*outs)
        flat = []
        for m in range(NM):
            flat += [view(m, res[m]), view(m, res[4 + m]), res[8 + m], res[12 + m]]
        return tuple(flat)

    return jax.shard_map(per_device, mesh=mesh, in_specs=in_specs, out_specs=out_specs, check_vma=False)
```

time: 58.2 us -> 57.4 us (0.986)
  Pallas kernels: 57.4 us -> 56.6 us
    pallas_call x1, Pallas kernels: 55.8 us -> 55 us  [per_device(): make_reduce_kernel(rows_b, cols, n_model, n_data)]
where the time goes in v5:
time: 57.4 us; the launch traced here: 57.2 us
  Pallas kernels  56.6 us (99%)
  between operations  0.66 us (1%)
    pallas_call x1, Pallas kernels, per_device(): make_reduce_kernel(rows_b, cols, n_model, n_data)  55 us
    pallas_call x1, Pallas kernels, per_device(): res = make_apply_kernel(rows_b, cols, n_model, n_data)(*outs)  1.57 us

profile of v5, /device:TPU:0, one launch (start us, length us, event | category | flops | bytes accessed | tf_op | source)
XLA Modules:
  0.0 57.2 jit_solution(13148935656060947679)
XLA Ops:
  0.7 55.0 %shard_map.279 = (f32[704,128]{1,0:T(8,128)S(1)}, f32[704,128]{1,0:T(8,128)S(1)}, f32[352,256]{1,0:T(8,128)S(1)}, f32[128,256]{1,0:T(8,128)S(1)}, f32[704,128]{1...) custom-call(f32[1,704,1024]{2,1,0:T(8,128)} %bitcast.8, ...), custom_call_target="tpu_custom_call" | custom-call | tf_op jit(solution)/shard_map/pallas_call | solution.py:509
  55.7 1.6 %shard_map.280 = (f32[704,128]{1,0:T(8,128)}, f32[704,128]{1,0:T(8,128)}, f32[352,256]{1,0:T(8,128)}, f32[128,256]{1,0:T(8,128)}, f32[704,128]{1,0:T(8,128)}, /*...) custom-call(f32[704,128]{1,0:T(8,128)S(1)} %get-tuple-element.41.ref, ...), custom_call_target="tpu_custom_call" | custom-call | tf_op jit(solution)/shard_map/pallas_call | solution.py:511

commit v6 on v5

--- a/solution.py
+++ b/solution.py
@@ -12,6 +12,7 @@
 OWN, NX, NY, ND = 0, 1, 2, 3
 FIRST_ROWS = 88
 PARTS = 4
+LEAD_NS = 200
 LANES = 128
 TILE = (8, LANES)
 MIB = 1024 * 1024
@@ -52,7 +53,12 @@
         take = lambda n: [sc.pop(0) for _ in range(n)]
         loc, rec, fxy, vrbuf, vcbuf = (take(4) for _ in range(5))
         stg, rmsg, rrx, cmsg, crx, csib, chalf, brx, vrc, vcc, stage, sent = take(12)
-        ld_sem, dd_r, l_r, ra_r, ca_r, cs_r, cm_r, b_r, s_sem, greet = take(10)
+        ld_sem, dd_r, l_r, half_r, s_sem, greet = take(6)
+        row_in = lambda m: ld_sem.at[m]
+        col_in = lambda m: half_r.at[m] if n_rc[m][1] == 8 else ld_sem.at[NM + m]
+        pair_in = lambda m: dd_r.at[m]
+        merge_in = lambda m: dd_r.at[2 + m]
+        totals_in = dd_r.at[NM]
 
         z = lax.axis_index('model')
         d = lax.axis_index('data')
@@ -180,13 +186,13 @@
             pl.semaphore_wait(barrier, 1)
             signal(barrier, data=dx + 1)
             signal(barrier, data=dy + 1)
-            signal(greet.at[2], data=sib)
+            signal(greet.at[3], data=sib)
 
         signal_z(barrier, data=sib, also=first_core)
 
         @pl.when(second_core)
         def _():
-            pl.semaphore_wait(greet.at[2], 1)
+            pl.semaphore_wait(greet.at[3], 1)
 
         for f in first:
             stage_in[f].wait()
@@ -195,18 +201,29 @@
         @pl.when(second_core)
         def _():
             pl.semaphore_wait(barrier, 2 + n_z)
-            signal(greet.at[3], data=sib)
+            signal(greet.at[4], data=sib)
 
         @pl.when(first_core)
         def _():
-            pl.semaphore_wait(greet.at[3], 1)
-
-        for i, f in enumerate(first):
-            loads[f].wait()
-            dsend[f].wait_recv()
+            pl.semaphore_wait(greet.at[4], 1)
+
+        def first_done(pieces):
+            for f in pieces:
+                loads[f].wait()
+                dsend[f].wait_recv()
+
+        @pl.when(second_core)
+        def _():
+            first_done(first[2:])
+            pl.delay(LEAD_NS)
+
+        first_done(first[:2])
+        for f in first[:2]:
             pair_sum(*f)
-            if i == 1:
-                fetch(group[0])
+        fetch(group[0])
+        pl.when(first_core)(lambda: first_done(first[2:]))
+        for f in first[2:]:
+            pair_sum(*f)
         fetch(group[1])
         send_raw(0)
         fetch(group[2])
@@ -266,36 +283,36 @@
                 vrc[m] = to_compact(2 * m, q['n0'])
                 vcc[m] = stage[2 * m + 1]
 
-        for i in range(2):
+        for i in range(3):
             signal_z(greet.at[i])
             pl.semaphore_wait(greet.at[i], n_z)
 
         def send_rows(m):
             n_r = n_rc[m][0]
             for k in (3, 2, 1):
-                remote(rmsg.at[m, pl.ds(0, n_r)], rrx.at[3 * m + k - 1, pl.ds(0, n_r)], s_sem.at[0], ra_r.at[m],
+                remote(rmsg.at[m, pl.ds(0, n_r)], rrx.at[3 * m + k - 1, pl.ds(0, n_r)], s_sem.at[0], row_in(m),
                        model=flip_z(k)).start()
 
         def send_cols(m, ks):
             n_c = n_rc[m][1]
             for k in ks:
-                remote(cmsg.at[m, pl.ds(0, n_c)], crx.at[7 * m + k - 1, pl.ds(0, n_c)], s_sem.at[0], ca_r.at[m],
+                remote(cmsg.at[m, pl.ds(0, n_c)], crx.at[7 * m + k - 1, pl.ds(0, n_c)], s_sem.at[0], col_in(m),
                        data=flip_d(k)).start()
 
         def share_pair(m):
-            wait_bytes(csib.at[m], cs_r.at[m])
+            wait_bytes(csib.at[m], pair_in(m))
             mine = jnp.where(core == 0, csib[m, 0:4, :] + cmsg[m, 0:4, :], csib[m, 4:8, :] + cmsg[m, 4:8, :])
             chalf[m, 0] = mine
             for k, peer in enumerate((dd, dx, dy)):
-                remote(chalf.at[m, 0], chalf.at[m, 1 + k], s_sem.at[0], ca_r.at[m], data=peer).start()
+                remote(chalf.at[m, 0], chalf.at[m, 1 + k], s_sem.at[0], col_in(m), data=peer).start()
 
         def merge_pair(m):
-            wait_bytes(chalf.at[m, pl.ds(1, 3)], ca_r.at[m])
+            wait_bytes(chalf.at[m, pl.ds(1, 3)], col_in(m))
             chalf[m, 4] = chalf[m, 0] + chalf[m, 1] + chalf[m, 2] + chalf[m, 3]
-            remote(chalf.at[m, 4], chalf.at[m, 5], s_sem.at[0], cm_r.at[m], data=sib).start()
+            remote(chalf.at[m, 4], chalf.at[m, 5], s_sem.at[0], merge_in(m), data=sib).start()
 
         def merged(m):
-            wait_bytes(chalf.at[m, 5], cm_r.at[m])
+            wait_bytes(chalf.at[m, 5], merge_in(m))
             mine, other = chalf[m, 4], chalf[m, 5]
             return jnp.concatenate([jnp.where(core == 0, mine, other), jnp.where(core == 0, other, mine)], axis=0)
 
@@ -322,7 +339,7 @@
             msg0[m] = compact(jnp.concatenate(rsums, axis=0))
             send_rows(m)
             if q['flip']:
-                remote(cmsg.at[m], csib.at[m], s_sem.at[0], cs_r.at[m], data=sib).start()
+                remote(cmsg.at[m], csib.at[m], s_sem.at[0], pair_in(m), data=sib).start()
 
         def apply_factors(m, bv, locrow):
             q = mats[m]
@@ -338,7 +355,7 @@
                 return jnp.concatenate(wide, axis=1)[None]
 
             rtot = rmsg[m, 0:n_r, :]
-            wait_bytes(loc[0].at[0, pl.ds(0, 3 * n_r), :], ra_r.at[m])
+            wait_bytes(loc[0].at[0, pl.ds(0, 3 * n_r), :], row_in(m))
             for k in range(3):
                 rtot = rtot + rrx[3 * m + k, 0:n_r, :]
             vr = BETA * vrc[m, 0:n_r, :] + (1.0 - BETA) * (rtot * (1.0 / q['cols_t']))
@@ -351,7 +368,7 @@
                 ctot = merged(m)
             else:
                 ctot = cmsg[m, 0:n_c, :]
-                wait_bytes(loc[0].at[0, pl.ds(0, 7 * n_c), :], ca_r.at[m])
+                wait_bytes(loc[0].at[0, pl.ds(0, 7 * n_c), :], col_in(m))
                 for k in range(7):
                     ctot = ctot + crx[7 * m + k, 0:n_c, :]
             vc = BETA * vcc[m, 0:n_c, :] + (1.0 - BETA) * (ctot * (1.0 / q['rows_t']))
@@ -392,7 +409,7 @@
                 if kz == 0 and kd == 0:
                     continue
                 i = kz * n_data + kd
-                remote(brx.at[pl.ds(0, 1), :], brx.at[pl.ds(i, 1), :], s_sem.at[0], b_r.at[0],
+                remote(brx.at[pl.ds(0, 1), :], brx.at[pl.ds(i, 1), :], s_sem.at[0], totals_in,
                        data=flip_d(kd), model=flip_z(kz)).start()
 
         for m in range(NM):
@@ -407,7 +424,7 @@
                 rows = jnp.sum(jnp.where(pick, wide[16 * t:16 * t + g_n], 0.0), axis=0)
                 stats[2 + 2 * m, t:t + 1, :] = jnp.sum(rows, axis=0, keepdims=True)
 
-        wait_bytes(brx.at[pl.ds(1, n_model * n_data - 1), :], b_r.at[0])
+        wait_bytes(brx.at[pl.ds(1, n_model * n_data - 1), :], totals_in)
         tot = jnp.broadcast_to(jnp.sum(brx[...], axis=0, keepdims=True), TILE)
         mean_vr = pltpu.roll(tot, LANES - NM, 1)
         u_rms = jnp.sqrt(mean_vr * tot)
@@ -429,8 +446,7 @@
     tile = lambda *lead: vm((*lead, 8, LANES), f32)
     scratch += [tile(NM), tile(3 * NM), tile(NM), tile(7 * NM), tile(2), vm((2, 6, 4, LANES), f32), vm((n_model * n_data, LANES), f32),
                 tile(NM), tile(NM), tile(2 * NM), vm((sent_rows, LANES), f32)]
-    scratch += [dma((8,)), dma((8,)), dma((2 * NM,)), dma((NM,)), dma((NM,)), dma((2,)), dma((2,)), dma((1,)), dma((1,)),
-                pltpu.SemaphoreType.REGULAR((4,))]
+    scratch += [dma((8,)), dma((8,)), dma((2 * NM,)), dma((2,)), dma((1,)), pltpu.SemaphoreType.REGULAR((5,))]
     blocks = [jax.ShapeDtypeStruct((q['n0'], q['n1']), f32) for q in mats]
     out_shape = blocks + blocks + [jax.ShapeDtypeStruct((1 + 2 * NM, 8, LANES), f32)]
     vmem = pl.BlockSpec(memory_space=pltpu.VMEM)

time: 57.4 us -> 57.1 us (level)
  no operation moved by 1% of the time
where the time goes in v6:
time: 57.1 us; the launch traced here: 56.9 us
  Pallas kernels  56.2 us (98%)
  between operations  0.66 us (1%)
    pallas_call x1, Pallas kernels, per_device(): make_reduce_kernel(rows_b, cols, n_model, n_data)  54.7 us
    pallas_call x1, Pallas kernels, per_device(): res = make_apply_kernel(rows_b, cols, n_model, n_data)(*outs)  1.57 us

profile of v6, /device:TPU:0, one launch (start us, length us, event | category | flops | bytes accessed | tf_op | source)
XLA Modules:
  0.0 56.9 jit_solution(10783808477217888025)
XLA Ops:
  0.7 54.7 %shard_map.279 = (f32[704,128]{1,0:T(8,128)S(1)}, f32[704,128]{1,0:T(8,128)S(1)}, f32[352,256]{1,0:T(8,128)S(1)}, f32[128,256]{1,0:T(8,128)S(1)}, f32[704,128]{1...) custom-call(f32[1,704,1024]{2,1,0:T(8,128)} %bitcast.8, ...), custom_call_target="tpu_custom_call" | custom-call | tf_op jit(solution)/shard_map/pallas_call | solution.py:525
  55.3 1.6 %shard_map.280 = (f32[704,128]{1,0:T(8,128)}, f32[704,128]{1,0:T(8,128)}, f32[352,256]{1,0:T(8,128)}, f32[128,256]{1,0:T(8,128)}, f32[704,128]{1,0:T(8,128)}, /*...) custom-call(f32[704,128]{1,0:T(8,128)S(1)} %get-tuple-element.41.ref, ...), custom_call_target="tpu_custom_call" | custom-call | tf_op jit(solution)/shard_map/pallas_call | solution.py:527

commit v7 on v6

--- a/solution.py
+++ b/solution.py
@@ -392,15 +392,15 @@
         share_pair(0)
         send_acc(2)
         finish_sum(1)
+        send_acc(3)
         share_pair(1)
-        send_acc(3)
         merge_pair(0)
         bv, locrow = apply_factors(0, bv, locrow)
         finish_sum(2)
+        finish_sum(3)
         merge_pair(1)
-        finish_sum(3)
+        bv, locrow = apply_factors(2, bv, locrow)
         bv, locrow = apply_factors(1, bv, locrow)
-        bv, locrow = apply_factors(2, bv, locrow)
         bv, locrow = apply_factors(3, bv, locrow)
 
         brx[0:1, :] = bv

time: 57.1 us -> 57 us (level)
  no operation moved by 1% of the time
where the time goes in v7:
time: 57 us; the launch traced here: 56.8 us
  Pallas kernels  56.1 us (98%)
  between operations  0.66 us (1%)
    pallas_call x1, Pallas kernels, per_device(): make_reduce_kernel(rows_b, cols, n_model, n_data)  54.6 us
    pallas_call x1, Pallas kernels, per_device(): res = make_apply_kernel(rows_b, cols, n_model, n_data)(*outs)  1.57 us

profile of v7, /device:TPU:0, one launch (start us, length us, event | category | flops | bytes accessed | tf_op | source)
XLA Modules:
  0.0 56.8 jit_solution(17802306093900587407)
XLA Ops:
  0.7 54.6 %shard_map.279 = (f32[704,128]{1,0:T(8,128)S(1)}, f32[704,128]{1,0:T(8,128)S(1)}, f32[352,256]{1,0:T(8,128)S(1)}, f32[128,256]{1,0:T(8,128)S(1)}, f32[704,128]{1...) custom-call(f32[1,704,1024]{2,1,0:T(8,128)} %bitcast.8, ...), custom_call_target="tpu_custom_call" | custom-call | tf_op jit(solution)/shard_map/pallas_call | solution.py:525
  55.2 1.6 %shard_map.280 = (f32[704,128]{1,0:T(8,128)}, f32[704,128]{1,0:T(8,128)}, f32[352,256]{1,0:T(8,128)}, f32[128,256]{1,0:T(8,128)}, f32[704,128]{1,0:T(8,128)}, /*...) custom-call(f32[704,128]{1,0:T(8,128)S(1)} %get-tuple-element.41.ref, ...), custom_call_target="tpu_custom_call" | custom-call | tf_op jit(solution)/shard_map/pallas_call | solution.py:527

commit v8 on v7

--- a/solution.py
+++ b/solution.py
@@ -53,9 +53,9 @@
         take = lambda n: [sc.pop(0) for _ in range(n)]
         loc, rec, fxy, vrbuf, vcbuf = (take(4) for _ in range(5))
         stg, rmsg, rrx, cmsg, crx, csib, chalf, brx, vrc, vcc, stage, sent = take(12)
-        ld_sem, dd_r, l_r, half_r, s_sem, greet = take(6)
+        ld_sem, dd_r, l_r, col_r, s_sem, greet = take(6)
         row_in = lambda m: ld_sem.at[m]
-        col_in = lambda m: half_r.at[m] if n_rc[m][1] == 8 else ld_sem.at[NM + m]
+        col_in = lambda m: col_r.at[m]
         pair_in = lambda m: dd_r.at[m]
         merge_in = lambda m: dd_r.at[2 + m]
         totals_in = dd_r.at[NM]
@@ -341,19 +341,17 @@
             if q['flip']:
                 remote(cmsg.at[m], csib.at[m], s_sem.at[0], pair_in(m), data=sib).start()
 
-        def apply_factors(m, bv, locrow):
-            q = mats[m]
-            n_r, n_c = n_rc[m]
-            g_n, n1 = q['groups'], q['n1']
-            ok = lane < g_n
-
-            def along0(fac):
-                return expand(fac, g_n)
-
-            def along1(fac):
-                wide = [jnp.broadcast_to(fac[k:k + 1, :], TILE) for k in range(q['lanes'])]
-                return jnp.concatenate(wide, axis=1)[None]
-
+        def along0(m, fac):
+            return expand(fac, mats[m]['groups'])
+
+        def along1(m, fac):
+            wide = [jnp.broadcast_to(fac[k:k + 1, :], TILE) for k in range(mats[m]['lanes'])]
+            return jnp.concatenate(wide, axis=1)[None]
+
+        def apply_rows(m, bv, locrow):
+            q = mats[m]
+            n_r = n_rc[m][0]
+            ok = lane < q['groups']
             rtot = rmsg[m, 0:n_r, :]
             wait_bytes(loc[0].at[0, pl.ds(0, 3 * n_r), :], row_in(m))
             for k in range(3):
@@ -361,9 +359,17 @@
             vr = BETA * vrc[m, 0:n_r, :] + (1.0 - BETA) * (rtot * (1.0 / q['cols_t']))
             vr_sum = jnp.sum(vr if q['flip'] else jnp.where(ok, vr, 0.0), axis=(0, 1), keepdims=True)
             mloc = vr_sum * (1.0 / q['rows_b'])
-            inv_mloc = 1.0 / mloc
             rfac = lax.rsqrt(vr / mloc) if q['flip'] else lax.rsqrt(jnp.where(ok, vr / mloc, 1.0))
-            part = upd[m][...].reshape(g_n, 8, n1) * (along1 if q['flip'] else along0)(rfac)
+            part = upd[m][...].reshape(q['groups'], 8, q['n1']) * (along1 if q['flip'] else along0)(m, rfac)
+            upd[m][...] = part.reshape(q['n0'], q['n1'])
+            vrc[m, 0:n_r, :] = vr
+            bv = jnp.where(lane1 == NM + m, vr_sum * (1.0 / (q['rows_t'] * n_model)), bv)
+            locrow = jnp.where(lane1 == m, mloc, locrow)
+            return bv, locrow, 1.0 / mloc
+
+        def apply_cols(m, bv, inv_mloc):
+            q = mats[m]
+            n_c = n_rc[m][1]
             if n_c == 8:
                 ctot = merged(m)
             else:
@@ -372,16 +378,12 @@
                 for k in range(7):
                     ctot = ctot + crx[7 * m + k, 0:n_c, :]
             vc = BETA * vcc[m, 0:n_c, :] + (1.0 - BETA) * (ctot * (1.0 / q['rows_t']))
-            cfac = lax.rsqrt(jnp.where(ok, vc, 1.0)) if q['flip'] else lax.rsqrt(vc)
-            u = part * (along0 if q['flip'] else along1)(cfac)
+            cfac = lax.rsqrt(jnp.where(lane < q['groups'], vc, 1.0)) if q['flip'] else lax.rsqrt(vc)
+            u = upd[m][...].reshape(q['groups'], 8, q['n1']) * (along0 if q['flip'] else along1)(m, cfac)
             t_m = jnp.sum(jnp.sum(u * u, axis=0), axis=(0, 1), keepdims=True)
-            upd[m][...] = u.reshape(q['n0'], n1)
-            vcc[m] = vc if q['flip'] else vr
-            stats[1 + 2 * m, 0:q['lanes'], :] = vr if q['flip'] else vc
-            bv = jnp.where(lane1 == NM + m, vr_sum * (1.0 / (q['rows_t'] * n_model)), bv)
-            bv = jnp.where(lane1 == m, (t_m * (1.0 / q['size'])) * inv_mloc, bv)
-            locrow = jnp.where(lane1 == m, mloc, locrow)
-            return bv, locrow
+            upd[m][...] = u.reshape(q['n0'], q['n1'])
+            vcc[m, 0:n_c, :] = vc
+            return jnp.where(lane1 == m, (t_m * (1.0 / q['size'])) * inv_mloc, bv)
 
         locrow = jnp.ones((1, LANES), jnp.float32)
         send_acc(0)
@@ -389,19 +391,23 @@
         send_acc(1)
         finish_sum(0)
         send_raw(3)
-        share_pair(0)
         send_acc(2)
         finish_sum(1)
         send_acc(3)
+        share_pair(0)
         share_pair(1)
-        merge_pair(0)
-        bv, locrow = apply_factors(0, bv, locrow)
+        bv, locrow, inv0 = apply_rows(0, bv, locrow)
+        bv, locrow, inv1 = apply_rows(1, bv, locrow)
         finish_sum(2)
         finish_sum(3)
+        merge_pair(0)
         merge_pair(1)
-        bv, locrow = apply_factors(2, bv, locrow)
-        bv, locrow = apply_factors(1, bv, locrow)
-        bv, locrow = apply_factors(3, bv, locrow)
+        bv, locrow, inv2 = apply_rows(2, bv, locrow)
+        bv = apply_cols(0, bv, inv0)
+        bv = apply_cols(1, bv, inv1)
+        bv = apply_cols(2, bv, inv2)
+        bv, locrow, inv3 = apply_rows(3, bv, locrow)
+        bv = apply_cols(3, bv, inv3)
 
         brx[0:1, :] = bv
         for kz in (3, 2, 1, 0):
@@ -414,7 +420,9 @@
 
         for m in range(NM):
             q = mats[m]
-            wide = expand(vcc[m], q['groups'])
+            lined, packed = (vrc, vcc) if q['flip'] else (vcc, vrc)
+            stats[1 + 2 * m, 0:q['lanes'], :] = lined[m, 0:q['lanes'], :]
+            wide = expand(packed[m], q['groups'])
             for t in range(q['tiles']):
                 n_t = min(LANES, q['n0'] - LANES * t)
                 g_n = n_t // 8
@@ -446,7 +454,7 @@
     tile = lambda *lead: vm((*lead, 8, LANES), f32)
     scratch += [tile(NM), tile(3 * NM), tile(NM), tile(7 * NM), tile(2), vm((2, 6, 4, LANES), f32), vm((n_model * n_data, LANES), f32),
                 tile(NM), tile(NM), tile(2 * NM), vm((sent_rows, LANES), f32)]
-    scratch += [dma((8,)), dma((8,)), dma((2 * NM,)), dma((2,)), dma((1,)), pltpu.SemaphoreType.REGULAR((5,))]
+    scratch += [dma((8,)), dma((8,)), dma((2 * NM,)), dma((NM,)), dma((1,)), pltpu.SemaphoreType.REGULAR((5,))]
     blocks = [jax.ShapeDtypeStruct((q['n0'], q['n1']), f32) for q in mats]
     out_shape = blocks + blocks + [jax.ShapeDtypeStruct((1 + 2 * NM, 8, LANES), f32)]
     vmem = pl.BlockSpec(memory_space=pltpu.VMEM)

time: 57 us -> 56.9 us (level)
  no operation moved by 1% of the time
where the time goes in v8:
time: 56.9 us; the launch traced here: 56.7 us
  Pallas kernels  56.1 us (99%)
  between operations  0.66 us (1%)
    pallas_call x1, Pallas kernels, per_device(): make_reduce_kernel(rows_b, cols, n_model, n_data)  54.5 us
    pallas_call x1, Pallas kernels, per_device(): res = make_apply_kernel(rows_b, cols, n_model, n_data)(*outs)  1.57 us

profile of v8, /device:TPU:0, one launch (start us, length us, event | category | flops | bytes accessed | tf_op | source)
XLA Modules:
  0.0 56.7 jit_solution(13909344902660836112)
XLA Ops:
  0.7 54.5 %shard_map.279 = (f32[704,128]{1,0:T(8,128)S(1)}, f32[704,128]{1,0:T(8,128)S(1)}, f32[352,256]{1,0:T(8,128)S(1)}, f32[128,256]{1,0:T(8,128)S(1)}, f32[704,128]{1...) custom-call(f32[1,704,1024]{2,1,0:T(8,128)} %bitcast.8, ...), custom_call_target="tpu_custom_call" | custom-call | tf_op jit(solution)/shard_map/pallas_call | solution.py:533
  55.2 1.6 %shard_map.280 = (f32[704,128]{1,0:T(8,128)}, f32[704,128]{1,0:T(8,128)}, f32[352,256]{1,0:T(8,128)}, f32[128,256]{1,0:T(8,128)}, f32[704,128]{1,0:T(8,128)}, /*...) custom-call(f32[704,128]{1,0:T(8,128)S(1)} %get-tuple-element.41.ref, ...), custom_call_target="tpu_custom_call" | custom-call | tf_op jit(solution)/shard_map/pallas_call | solution.py:535

commit v9 on v8

--- a/solution.py
+++ b/solution.py
@@ -201,11 +201,11 @@
         @pl.when(second_core)
         def _():
             pl.semaphore_wait(barrier, 2 + n_z)
-            signal(greet.at[4], data=sib)
+            signal(greet.at[3], data=sib)
 
         @pl.when(first_core)
         def _():
-            pl.semaphore_wait(greet.at[4], 1)
+            pl.semaphore_wait(greet.at[3], 1)
 
         def first_done(pieces):
             for f in pieces:
@@ -411,7 +411,7 @@
 
         brx[0:1, :] = bv
         for kz in (3, 2, 1, 0):
-            for kd in range(n_data - 1, -1, -1):
+            for kd in (6, 7, 2, 4, 0, 3, 5, 1):
                 if kz == 0 and kd == 0:
                     continue
                 i = kz * n_data + kd
@@ -454,7 +454,7 @@
     tile = lambda *lead: vm((*lead, 8, LANES), f32)
     scratch += [tile(NM), tile(3 * NM), tile(NM), tile(7 * NM), tile(2), vm((2, 6, 4, LANES), f32), vm((n_model * n_data, LANES), f32),
                 tile(NM), tile(NM), tile(2 * NM), vm((sent_rows, LANES), f32)]
-    scratch += [dma((8,)), dma((8,)), dma((2 * NM,)), dma((NM,)), dma((1,)), pltpu.SemaphoreType.REGULAR((5,))]
+    scratch += [dma((8,)), dma((8,)), dma((2 * NM,)), dma((NM,)), dma((1,)), pltpu.SemaphoreType.REGULAR((4,))]
     blocks = [jax.ShapeDtypeStruct((q['n0'], q['n1']), f32) for q in mats]
     out_shape = blocks + blocks + [jax.ShapeDtypeStruct((1 + 2 * NM, 8, LANES), f32)]
     vmem = pl.BlockSpec(memory_space=pltpu.VMEM)
@@ -473,7 +473,7 @@
         upd, params, stats = refs[0:4], refs[4:8], refs[8]
         new, delta, vrow_out, vcol_out = refs[9:13], refs[13:17], refs[17:21], refs[21:25]
         bufs, vrbuf, vcbuf = refs[25:29], refs[29:33], refs[33:37]
-        sem = refs[37]
+        out_bytes, sem = refs[37:39]
         for m in range(NM):
             fac = stats[0, 0:1, m:m + 1]
             n = mats[m]['n0'] // PARTS
@@ -481,9 +481,9 @@
                 rows = slice(i * n, i * n + n)
                 step = fac * upd[m][rows, :]
                 bufs[m][0, rows, :] = step
-                pltpu.make_async_copy(bufs[m].at[0, rows], delta[m].at[rows], sem.at[m]).start()
+                pltpu.make_async_copy(bufs[m].at[0, rows], delta[m].at[rows], sem.at[0]).start()
                 bufs[m][1, rows, :] = params[m][rows, :] + step
-                pltpu.make_async_copy(bufs[m].at[1, rows], new[m].at[rows], sem.at[m]).start()
+                pltpu.make_async_copy(bufs[m].at[1, rows], new[m].at[rows], sem.at[0]).start()
         copies = []
         for m in range(NM):
             q = mats[m]
@@ -494,10 +494,9 @@
                 n_t = min(LANES, q['n0'] - LANES * t)
                 out0[pl.ds(LANES * t, n_t)] = stats[2 + 2 * m, t:t + 1, 0:n_t].reshape(n_t)
             for i, (buf, out) in enumerate(((vrbuf[m], vrow_out[m]), (vcbuf[m], vcol_out[m]))):
-                copies.append(pltpu.make_async_copy(buf, out, sem.at[NM + 2 * m + i]))
+                copies.append(pltpu.make_async_copy(buf, out, sem.at[1 + 2 * m + i]))
                 copies[-1].start()
-        for m in range(NM):
-            pltpu.make_async_copy(bufs[m], bufs[m], sem.at[m]).wait()
+        pltpu.make_async_copy(out_bytes, out_bytes, sem.at[0]).wait()
         for cp in copies:
             cp.wait()
 
@@ -505,13 +504,14 @@
     vmem = pl.BlockSpec(memory_space=pltpu.VMEM)
     hbm = pl.BlockSpec(memory_space=pltpu.HBM)
     blocks = [jax.ShapeDtypeStruct((q['n0'], q['n1']), f32) for q in mats]
+    out_rows = sum(2 * q['n0'] * q['lanes'] for q in mats)
     out_shape = (blocks + blocks + [jax.ShapeDtypeStruct((r,), f32) for r in rows_b]
                  + [jax.ShapeDtypeStruct((c,), f32) for c in cols])
     scratch = [pltpu.VMEM((2, q['n0'], q['n1']), f32) for q in mats]
-    scratch += [pltpu.VMEM((n,), f32) for n in (*rows_b, *cols)] + [pltpu.SemaphoreType.DMA((3 * NM,))]
+    scratch += [pltpu.VMEM((n,), f32) for n in (*rows_b, *cols)] + [pltpu.VMEM((out_rows, LANES), f32), pltpu.SemaphoreType.DMA((1 + 2 * NM,))]
     return pl.pallas_call(
         kernel, out_shape=out_shape, in_specs=[vmem] * 9, out_specs=[hbm] * 16, scratch_shapes=scratch,
-        compiler_params=pltpu.CompilerParams(vmem_limit_bytes=6 * MIB))
+        compiler_params=pltpu.CompilerParams(vmem_limit_bytes=8 * MIB))
 
 
 def solution(mesh):

time: 56.9 us -> 56.9 us (level)
  no operation moved by 1% of the time
where the time goes in v9:
time: 56.9 us; the launch traced here: 56.7 us
  Pallas kernels  56 us (98%)
  between operations  0.66 us (1%)
    pallas_call x1, Pallas kernels, per_device(): make_reduce_kernel(rows_b, cols, n_model, n_data)  54.5 us
    pallas_call x1, Pallas kernels, per_device(): res = make_apply_kernel(rows_b, cols, n_model, n_data)(*outs)  1.54 us

profile of v9, /device:TPU:0, one launch (start us, length us, event | category | flops | bytes accessed | tf_op | source)
XLA Modules:
  0.0 56.7 jit_solution(15024650328187415940)
XLA Ops:
  0.7 54.5 %shard_map.279 = (f32[704,128]{1,0:T(8,128)S(1)}, f32[704,128]{1,0:T(8,128)S(1)}, f32[352,256]{1,0:T(8,128)S(1)}, f32[128,256]{1,0:T(8,128)S(1)}, f32[704,128]{1...) custom-call(f32[1,704,1024]{2,1,0:T(8,128)} %bitcast.8, ...), custom_call_target="tpu_custom_call" | custom-call | tf_op jit(solution)/shard_map/pallas_call | solution.py:533
  55.1 1.5 %shard_map.280 = (f32[704,128]{1,0:T(8,128)}, f32[704,128]{1,0:T(8,128)}, f32[352,256]{1,0:T(8,128)}, f32[128,256]{1,0:T(8,128)}, f32[704,128]{1,0:T(8,128)}, /*...) custom-call(f32[704,128]{1,0:T(8,128)S(1)} %get-tuple-element.41.ref, ...), custom_call_target="tpu_custom_call" | custom-call | tf_op jit(solution)/shard_map/pallas_call | solution.py:535

commit v10 on v9

--- a/solution.py
+++ b/solution.py
@@ -55,7 +55,8 @@
         stg, rmsg, rrx, cmsg, crx, csib, chalf, brx, vrc, vcc, stage, sent = take(12)
         ld_sem, dd_r, l_r, col_r, s_sem, greet = take(6)
         row_in = lambda m: ld_sem.at[m]
-        col_in = lambda m: col_r.at[m]
+        col_in = lambda m: (col_r.at[0], col_r.at[1], dd_r.at[NM + 1], col_r.at[2])[m]
+        link_in = lambda m, final: l_r.at[2 * m + final] if m < NM - 1 else ld_sem.at[NM + final]
         pair_in = lambda m: dd_r.at[m]
         merge_in = lambda m: dd_r.at[2 + m]
         totals_in = dd_r.at[NM]
@@ -147,13 +148,13 @@
             along_x = (j == ND and h == 0) or j == NX
             slot = (0 if along_x else 1) if j == ND else (2 if along_x else 4) + h
             return remote(loc[m].at[j, pl.ds(r0, n), :], fxy[m].at[slot, pl.ds(off, n), :],
-                          s_sem.at[0], l_r.at[2 * m + (0 if j == ND else 1)], data=dx if along_x else dy)
+                          s_sem.at[0], link_in(m, int(j != ND)), data=dx if along_x else dy)
 
         def relays_in(m):
-            wait_bytes(fxy[m].at[pl.ds(0, 2)], l_r.at[2 * m])
+            wait_bytes(fxy[m].at[pl.ds(0, 2)], link_in(m, 0))
 
         def finals_in(m):
-            wait_bytes(fxy[m].at[pl.ds(2, 4)], l_r.at[2 * m + 1])
+            wait_bytes(fxy[m].at[pl.ds(2, 4)], link_in(m, 1))
 
         def pair_sum(m, j, r0, n, relay=None):
             total = loc[m][j, r0:r0 + n, :] + rec[m][j, r0:r0 + n, :]
@@ -322,10 +323,11 @@
             half, n1 = q['half'], q['n1']
             acc1 = jnp.zeros((8, n1), jnp.float32)
             rsums = []
+            loc[m][OWN] = loc[m][OWN] + rec[m][OWN]
             finals_in(m)
             for h in range(2):
                 rows = slice(h * half, (h + 1) * half)
-                total = loc[m][OWN, rows, :] + rec[m][OWN, rows, :] + fxy[m][2 + h] + fxy[m][4 + h]
+                total = loc[m][OWN, rows, :] + fxy[m][2 + h] + fxy[m][4 + h]
                 upd[m][rows, :] = total
                 sq = (total * total + 1e-30).reshape(half // 8, 8, n1)
                 acc1 = acc1 + jnp.sum(sq, axis=0)
@@ -454,7 +456,7 @@
     tile = lambda *lead: vm((*lead, 8, LANES), f32)
     scratch += [tile(NM), tile(3 * NM), tile(NM), tile(7 * NM), tile(2), vm((2, 6, 4, LANES), f32), vm((n_model * n_data, LANES), f32),
                 tile(NM), tile(NM), tile(2 * NM), vm((sent_rows, LANES), f32)]
-    scratch += [dma((8,)), dma((8,)), dma((2 * NM,)), dma((NM,)), dma((1,)), pltpu.SemaphoreType.REGULAR((4,))]
+    scratch += [dma((8,)), dma((8,)), dma((2 * NM - 2,)), dma((NM - 1,)), dma((1,)), pltpu.SemaphoreType.REGULAR((4,))]
     blocks = [jax.ShapeDtypeStruct((q['n0'], q['n1']), f32) for q in mats]
     out_shape = blocks + blocks + [jax.ShapeDtypeStruct((1 + 2 * NM, 8, LANES), f32)]
     vmem = pl.BlockSpec(memory_space=pltpu.VMEM)

time: 56.9 us -> 56.9 us (level)
  no operation moved by 1% of the time
where the time goes in v10:
time: 56.9 us; the launch traced here: 56.7 us
  Pallas kernels  56 us (98%)
  between operations  0.66 us (1%)
    pallas_call x1, Pallas kernels, per_device(): make_reduce_kernel(rows_b, cols, n_model, n_data)  54.5 us
    pallas_call x1, Pallas kernels, per_device(): res = make_apply_kernel(rows_b, cols, n_model, n_data)(*outs)  1.54 us

profile of v10, /device:TPU:0, one launch (start us, length us, event | category | flops | bytes accessed | tf_op | source)
XLA Modules:
  0.0 56.7 jit_solution(125762005652654408)
XLA Ops:
  0.7 54.5 %shard_map.279 = (f32[704,128]{1,0:T(8,128)S(1)}, f32[704,128]{1,0:T(8,128)S(1)}, f32[352,256]{1,0:T(8,128)S(1)}, f32[128,256]{1,0:T(8,128)S(1)}, f32[704,128]{1...) custom-call(f32[1,704,1024]{2,1,0:T(8,128)} %bitcast.8, ...), custom_call_target="tpu_custom_call" | custom-call | tf_op jit(solution)/shard_map/pallas_call | solution.py:535
  55.1 1.5 %shard_map.280 = (f32[704,128]{1,0:T(8,128)}, f32[704,128]{1,0:T(8,128)}, f32[352,256]{1,0:T(8,128)}, f32[128,256]{1,0:T(8,128)}, f32[704,128]{1,0:T(8,128)}, /*...) custom-call(f32[704,128]{1,0:T(8,128)S(1)} %get-tuple-element.41.ref, ...), custom_call_target="tpu_custom_call" | custom-call | tf_op jit(solution)/shard_map/pallas_call | solution.py:537

commit v11 on v10

--- a/solution.py
+++ b/solution.py
@@ -11,7 +11,7 @@
 NM = 4
 OWN, NX, NY, ND = 0, 1, 2, 3
 FIRST_ROWS = 88
-PARTS = 4
+PARTS = (8, 4, 4, 4)
 LEAD_NS = 200
 LANES = 128
 TILE = (8, LANES)
@@ -216,7 +216,10 @@
         @pl.when(second_core)
         def _():
             first_done(first[2:])
-            pl.delay(LEAD_NS)
+
+            @pl.when(xx + yy < 2)
+            def _():
+                pl.delay(LEAD_NS)
 
         first_done(first[:2])
         for f in first[:2]:
@@ -478,8 +481,8 @@
         out_bytes, sem = refs[37:39]
         for m in range(NM):
             fac = stats[0, 0:1, m:m + 1]
-            n = mats[m]['n0'] // PARTS
-            for i in range(PARTS):
+            n = mats[m]['n0'] // PARTS[m]
+            for i in range(PARTS[m]):
                 rows = slice(i * n, i * n + n)
                 step = fac * upd[m][rows, :]
                 bufs[m][0, rows, :] = step

time: 56.9 us -> 56.9 us (level)
  no operation moved by 1% of the time
where the time goes in v11:
time: 56.9 us; the launch traced here: 56.6 us
  Pallas kernels  56 us (98%)
  between operations  0.66 us (1%)
    pallas_call x1, Pallas kernels, per_device(): make_reduce_kernel(rows_b, cols, n_model, n_data)  54.4 us
    pallas_call x1, Pallas kernels, per_device(): res = make_apply_kernel(rows_b, cols, n_model, n_data)(*outs)  1.54 us

profile of v11, /device:TPU:0, one launch (start us, length us, event | category | flops | bytes accessed | tf_op | source)
XLA Modules:
  0.0 56.6 jit_solution(10153480827934422140)
XLA Ops:
  0.7 54.4 %shard_map.279 = (f32[704,128]{1,0:T(8,128)S(1)}, f32[704,128]{1,0:T(8,128)S(1)}, f32[352,256]{1,0:T(8,128)S(1)}, f32[128,256]{1,0:T(8,128)S(1)}, f32[704,128]{1...) custom-call(f32[1,704,1024]{2,1,0:T(8,128)} %bitcast.8, ...), custom_call_target="tpu_custom_call" | custom-call | tf_op jit(solution)/shard_map/pallas_call | solution.py:538
  55.1 1.5 %shard_map.280 = (f32[704,128]{1,0:T(8,128)}, f32[704,128]{1,0:T(8,128)}, f32[352,256]{1,0:T(8,128)}, f32[128,256]{1,0:T(8,128)}, f32[704,128]{1,0:T(8,128)}, /*...) custom-call(f32[704,128]{1,0:T(8,128)S(1)} %get-tuple-element.41.ref, ...), custom_call_target="tpu_custom_call" | custom-call | tf_op jit(solution)/shard_map/pallas_call | solution.py:540
